TPU v7x, 32 devices: a whole 2x2x4 slice. The times are simulated.
32 devices in a mesh: data: 4 (over x, y), stage: 8 (over z, core).
Axes of the slice: x: 2, y: 2, z: 4, core: 2. Of those that a mesh axis runs over, the one named last changes fastest.
Arguments:
- X: bfloat16 [32, 256, 768], P('data'), parts along dimension 0
- G: bfloat16 [32, 256, 768], P('data'), parts along dimension 0
- W1: bfloat16 [8, 768, 3072], P('stage')
- W2: bfloat16 [8, 3072, 768], P('stage')
Outputs:
- output 1: bfloat16 [32, 256, 768], P('data'), parts along dimension 0
- output 2: bfloat16 [32, 256, 768], P('data'), parts along dimension 0
- output 3: float32 [32, 768, 3072], P(('data', 'stage')), parts along dimension 0
- output 4: float32 [32, 3072, 768], P(('data', 'stage')), parts along dimension 0
There are 4 independent parts. A program takes and returns all parts, laid end to end along the dimension named above; an argument that names none is the same for every part.
All inputs are finite; a program needn't handle non-finite values.
Results may differ from a plain program's by a relative error of at most 0.0131113.
Values are sent between devices in bfloat16 or wider.
A program may use at most 1 GiB of HBM per device.

v0:
```python
import jax
import jax.numpy as jnp
from jax import lax
from jax.sharding import PartitionSpec as P


def _fwd_layer(h, w1, w2):
    z = jnp.dot(h, w1, preferred_element_type=jnp.float32)
    u = jax.nn.gelu(z, approximate=True).astype(jnp.bfloat16)
    return (h.astype(jnp.float32) + jnp.dot(u, w2, preferred_element_type=jnp.float32)).astype(jnp.bfloat16)


def _bwd_layer(h, g, w1, w2):
    z = jnp.dot(h, w1, preferred_element_type=jnp.float32)
    u, gelu_vjp = jax.vjp(lambda t: jax.nn.gelu(t, approximate=True), z)
    du = jnp.dot(g, w2.T, preferred_element_type=jnp.float32)
    dz = gelu_vjp(du)[0].astype(jnp.bfloat16)
    dw2 = jnp.dot(u.astype(jnp.bfloat16).T, g, preferred_element_type=jnp.float32)
    dw1 = jnp.dot(h.T, dz, preferred_element_type=jnp.float32)
    dh = (g.astype(jnp.float32) + jnp.dot(dz, w1.T, preferred_element_type=jnp.float32)).astype(jnp.bfloat16)
    return dh, dw1, dw2


def _put(buf, i, val, ok):
    old = lax.dynamic_index_in_dim(buf, i, 0, keepdims=False)
    return lax.dynamic_update_index_in_dim(buf, jnp.where(ok, val, old), i, 0)


def solution(mesh):
    n_st = mesh.shape['stage']
    fwd_perm = [(i, i + 1) for i in range(n_st - 1)]
    bwd_perm = [(i + 1, i) for i in range(n_st - 1)]

    def body(x, g, w1, w2):
        s = lax.axis_index('stage')
        n_mb = x.shape[0]
        lps = w1.shape[0]
        first = s == 0
        last = s == n_st - 1
        ticks = n_mb + n_st - 1
        mb_shape = x.shape[1:]

        def fwd_tick(t, carry):
            recv, saved, y = carry
            m = t - s
            ok = (m >= 0) & (m < n_mb)
            mc = jnp.clip(m, 0, n_mb - 1)
            h = jnp.where(first, lax.dynamic_index_in_dim(x, mc, 0, keepdims=False), recv)
            hs = []
            for j in range(lps):
                hs.append(h)
                h = _fwd_layer(h, w1[j], w2[j])
            saved = _put(saved, mc, jnp.stack(hs), ok)
            y = _put(y, mc, h, ok & last)
            recv = lax.ppermute(h, 'stage', fwd_perm)
            return recv, saved, y

        recv0 = jnp.zeros(mb_shape, x.dtype)
        saved0 = jnp.zeros((n_mb, lps) + mb_shape, x.dtype)
        _, saved, y = lax.fori_loop(0, ticks, fwd_tick, (recv0, saved0, jnp.zeros_like(x)))

        def bwd_tick(t, carry):
            recv, dx, a1, a2 = carry
            m = t - (n_st - 1 - s)
            ok = (m >= 0) & (m < n_mb)
            mc = jnp.clip(m, 0, n_mb - 1)
            gh = jnp.where(last, lax.dynamic_index_in_dim(g, mc, 0, keepdims=False), recv)
            hs = lax.dynamic_index_in_dim(saved, mc, 0, keepdims=False)
            a1 = list(a1)
            a2 = list(a2)
            for j in reversed(range(lps)):
                gh, dw1, dw2 = _bwd_layer(hs[j], gh, w1[j], w2[j])
                a1[j] = a1[j] + jnp.where(ok, dw1, 0.0)
                a2[j] = a2[j] + jnp.where(ok, dw2, 0.0)
            dx = _put(dx, mc, gh, ok & first)
            recv = lax.ppermute(gh, 'stage', bwd_perm)
            return recv, dx, tuple(a1), tuple(a2)

        a10 = tuple(jnp.zeros(w1.shape[1:], jnp.float32) for _ in range(lps))
        a20 = tuple(jnp.zeros(w2.shape[1:], jnp.float32) for _ in range(lps))
        _, dx, a1, a2 = lax.fori_loop(0, ticks, bwd_tick, (recv0, jnp.zeros_like(x), a10, a20))
        y = lax.psum(y, 'stage')
        dx = lax.psum(dx, 'stage')
        return y, dx, jnp.stack(a1), jnp.stack(a2)

    return jax.shard_map(body, mesh=mesh,
                         in_specs=(P('data'), P('data'), P('stage'), P('stage')),
                         out_specs=(P('data'), P('data'), P(('data', 'stage')), P(('data', 'stage'))),
                         check_vma=False)
```

profile of v0, /device:TPU:0, one launch (start us, length us, event | category | flops | bytes accessed | tf_op | source)
XLA Modules:
  0.0 926.7 jit_solution(699212386939256708)
XLA Ops:
  9.4 275.7 %while.39 = (s32[]{:T(128)}, bf16[256,768]{1,0:T(8,128)(2,1)S(1)}, bf16[8,1,256,768]{3,2,1,0:T(8,128)(2,1)}, bf16[8,256,768]{2,1,0:T(8,128)(2,1)S(1)}, pred[]{:T...) while((s32[]{:T(128)}, bf16[256,768]{1,0:T(8,128)(2,1)S(1)}, ...), condition=%wide.region_1.2_spmd, body=%wide.region_0.1_spmd.sunk | while | flops 2424569856 | bytes 17698036 | solution.py:60
  10.1 7.7 bitcast_dynamic-update-slice_fusion.6
  25.7 7.7 bitcast_dynamic-update-slice_fusion.6
  33.4 6.3 collective-permute-start
  44.5 7.7 bitcast_dynamic-update-slice_fusion.6
  52.2 6.2 collective-permute-start
  63.0 7.7 bitcast_dynamic-update-slice_fusion.6
  70.7 6.2 collective-permute-start
  81.6 7.7 bitcast_dynamic-update-slice_fusion.6
  89.3 6.2 collective-permute-start
  100.1 7.7 bitcast_dynamic-update-slice_fusion.6
  107.9 6.2 collective-permute-start
  118.7 7.7 bitcast_dynamic-update-slice_fusion.6
  126.4 6.2 collective-permute-start
  137.3 7.7 bitcast_dynamic-update-slice_fusion.6
  145.0 6.2 collective-permute-start
  155.8 7.7 bitcast_dynamic-update-slice_fusion.6
  163.6 6.2 collective-permute-start
  174.4 7.7 bitcast_dynamic-update-slice_fusion.6
  182.1 6.2 collective-permute-start
  193.0 7.7 bitcast_dynamic-update-slice_fusion.6
  200.7 6.2 collective-permute-start
  211.5 7.7 bitcast_dynamic-update-slice_fusion.6
  219.3 6.2 collective-permute-start
  230.1 7.7 bitcast_dynamic-update-slice_fusion.6
  237.8 6.2 collective-permute-start
  248.7 7.7 bitcast_dynamic-update-slice_fusion.6
  256.4 6.2 collective-permute-start
  267.2 7.7 bitcast_dynamic-update-slice_fusion.6
  275.0 6.2 collective-permute-start
  287.7 474.3 %while.40 = (s32[]{:T(128)}, bf16[256,768]{1,0:T(8,128)(2,1)S(1)}, bf16[8,256,768]{2,1,0:T(8,128)(2,1)}, f32[768,3072]{1,0:T(8,128)}, f32[3072,768]{1,0:T(8,128)...) while((s32[]{:T(128)}, bf16[256,768]{1,0:T(8,128)(2,1)S(1)}, ...), condition=%wide.region_4.5_spmd.clone, body=%wide.region_3.4_spmd.clone.sunk | while | flops 6077743104 | bytes 179700240 | solution.py:81
  301.2 8.2 select_add_fusion.5
  318.0 4.1 fusion.91
  330.3 10.9 %select_add_fusion.5 = f32[3072,768]{1,0:T(8,128)} fusion(f32[3072,768]{1,0:T(8,128)} %get-tuple-element.762, bf16[256,768]{1,0:T(8,128)(2,1)S(1)} %bitcast_select_fusion.12, pred[]{:T(512)S(6)} %compare.3, pred[]{:T(512)S(6)} %and.43, f32[256,3072]{1,0:T(8,128)} %copy-done.1), kind=kOutput, calls=%fused_computation.27.clone.1 | convolution fusion | flops 1222115328 | bytes 22413314 | tf_op jit(solution)/shard_map/while/body/eval_jaxpr/dot_general | solution.py:18
  362.1 10.9 %select_add_fusion.5 = f32[3072,768]{1,0:T(8,128)} fusion(f32[3072,768]{1,0:T(8,128)} %get-tuple-element.762, bf16[256,768]{1,0:T(8,128)(2,1)S(1)} %bitcast_select_fusion.12, pred[]{:T(512)S(6)} %compare.3, pred[]{:T(512)S(6)} %and.43, f32[256,3072]{1,0:T(8,128)} %copy-done.1), kind=kOutput, calls=%fused_computation.27.clone.1 | convolution fusion | flops 1222115328 | bytes 22413314 | tf_op jit(solution)/shard_map/while/body/eval_jaxpr/dot_general | solution.py:18
  393.9 10.9 %select_add_fusion.5 = f32[3072,768]{1,0:T(8,128)} fusion(f32[3072,768]{1,0:T(8,128)} %get-tuple-element.762, bf16[256,768]{1,0:T(8,128)(2,1)S(1)} %bitcast_select_fusion.12, pred[]{:T(512)S(6)} %compare.3, pred[]{:T(512)S(6)} %and.43, f32[256,3072]{1,0:T(8,128)} %copy-done.1), kind=kOutput, calls=%fused_computation.27.clone.1 | convolution fusion | flops 1222115328 | bytes 22413314 | tf_op jit(solution)/shard_map/while/body/eval_jaxpr/dot_general | solution.py:18
  425.8 10.9 %select_add_fusion.5 = f32[3072,768]{1,0:T(8,128)} fusion(f32[3072,768]{1,0:T(8,128)} %get-tuple-element.762, bf16[256,768]{1,0:T(8,128)(2,1)S(1)} %bitcast_select_fusion.12, pred[]{:T(512)S(6)} %compare.3, pred[]{:T(512)S(6)} %and.43, f32[256,3072]{1,0:T(8,128)} %copy-done.1), kind=kOutput, calls=%fused_computation.27.clone.1 | convolution fusion | flops 1222115328 | bytes 22413314 | tf_op jit(solution)/shard_map/while/body/eval_jaxpr/dot_general | solution.py:18
  457.6 10.9 %select_add_fusion.5 = f32[3072,768]{1,0:T(8,128)} fusion(f32[3072,768]{1,0:T(8,128)} %get-tuple-element.762, bf16[256,768]{1,0:T(8,128)(2,1)S(1)} %bitcast_select_fusion.12, pred[]{:T(512)S(6)} %compare.3, pred[]{:T(512)S(6)} %and.43, f32[256,3072]{1,0:T(8,128)} %copy-done.1), kind=kOutput, calls=%fused_computation.27.clone.1 | convolution fusion | flops 1222115328 | bytes 22413314 | tf_op jit(solution)/shard_map/while/body/eval_jaxpr/dot_general | solution.py:18
  489.4 10.9 %select_add_fusion.5 = f32[3072,768]{1,0:T(8,128)} fusion(f32[3072,768]{1,0:T(8,128)} %get-tuple-element.762, bf16[256,768]{1,0:T(8,128)(2,1)S(1)} %bitcast_select_fusion.12, pred[]{:T(512)S(6)} %compare.3, pred[]{:T(512)S(6)} %and.43, f32[256,3072]{1,0:T(8,128)} %copy-done.1), kind=kOutput, calls=%fused_computation.27.clone.1 | convolution fusion | flops 1222115328 | bytes 22413314 | tf_op jit(solution)/shard_map/while/body/eval_jaxpr/dot_general | solution.py:18
  521.2 10.9 %select_add_fusion.5 = f32[3072,768]{1,0:T(8,128)} fusion(f32[3072,768]{1,0:T(8,128)} %get-tuple-element.762, bf16[256,768]{1,0:T(8,128)(2,1)S(1)} %bitcast_select_fusion.12, pred[]{:T(512)S(6)} %compare.3, pred[]{:T(512)S(6)} %and.43, f32[256,3072]{1,0:T(8,128)} %copy-done.1), kind=kOutput, calls=%fused_computation.27.clone.1 | convolution fusion | flops 1222115328 | bytes 22413314 | tf_op jit(solution)/shard_map/while/body/eval_jaxpr/dot_general | solution.py:18
  553.0 10.9 %select_add_fusion.5 = f32[3072,768]{1,0:T(8,128)} fusion(f32[3072,768]{1,0:T(8,128)} %get-tuple-element.762, bf16[256,768]{1,0:T(8,128)(2,1)S(1)} %bitcast_select_fusion.12, pred[]{:T(512)S(6)} %compare.3, pred[]{:T(512)S(6)} %and.43, f32[256,3072]{1,0:T(8,128)} %copy-done.1), kind=kOutput, calls=%fused_computation.27.clone.1 | convolution fusion | flops 1222115328 | bytes 22413314 | tf_op jit(solution)/shard_map/while/body/eval_jaxpr/dot_general | solution.py:18
  584.8 10.9 %select_add_fusion.5 = f32[3072,768]{1,0:T(8,128)} fusion(f32[3072,768]{1,0:T(8,128)} %get-tuple-element.762, bf16[256,768]{1,0:T(8,128)(2,1)S(1)} %bitcast_select_fusion.12, pred[]{:T(512)S(6)} %compare.3, pred[]{:T(512)S(6)} %and.43, f32[256,3072]{1,0:T(8,128)} %copy-done.1), kind=kOutput, calls=%fused_computation.27.clone.1 | convolution fusion | flops 1222115328 | bytes 22413314 | tf_op jit(solution)/shard_map/while/body/eval_jaxpr/dot_general | solution.py:18
  616.6 10.9 %select_add_fusion.5 = f32[3072,768]{1,0:T(8,128)} fusion(f32[3072,768]{1,0:T(8,128)} %get-tuple-element.762, bf16[256,768]{1,0:T(8,128)(2,1)S(1)} %bitcast_select_fusion.12, pred[]{:T(512)S(6)} %compare.3, pred[]{:T(512)S(6)} %and.43, f32[256,3072]{1,0:T(8,128)} %copy-done.1), kind=kOutput, calls=%fused_computation.27.clone.1 | convolution fusion | flops 1222115328 | bytes 22413314 | tf_op jit(solution)/shard_map/while/body/eval_jaxpr/dot_general | solution.py:18
  648.4 10.9 %select_add_fusion.5 = f32[3072,768]{1,0:T(8,128)} fusion(f32[3072,768]{1,0:T(8,128)} %get-tuple-element.762, bf16[256,768]{1,0:T(8,128)(2,1)S(1)} %bitcast_select_fusion.12, pred[]{:T(512)S(6)} %compare.3, pred[]{:T(512)S(6)} %and.43, f32[256,3072]{1,0:T(8,128)} %copy-done.1), kind=kOutput, calls=%fused_computation.27.clone.1 | convolution fusion | flops 1222115328 | bytes 22413314 | tf_op jit(solution)/shard_map/while/body/eval_jaxpr/dot_general | solution.py:18
  680.2 10.9 %select_add_fusion.5 = f32[3072,768]{1,0:T(8,128)} fusion(f32[3072,768]{1,0:T(8,128)} %get-tuple-element.762, bf16[256,768]{1,0:T(8,128)(2,1)S(1)} %bitcast_select_fusion.12, pred[]{:T(512)S(6)} %compare.3, pred[]{:T(512)S(6)} %and.43, f32[256,3072]{1,0:T(8,128)} %copy-done.1), kind=kOutput, calls=%fused_computation.27.clone.1 | convolution fusion | flops 1222115328 | bytes 22413314 | tf_op jit(solution)/shard_map/while/body/eval_jaxpr/dot_general | solution.py:18
  712.0 10.9 %select_add_fusion.5 = f32[3072,768]{1,0:T(8,128)} fusion(f32[3072,768]{1,0:T(8,128)} %get-tuple-element.762, bf16[256,768]{1,0:T(8,128)(2,1)S(1)} %bitcast_select_fusion.12, pred[]{:T(512)S(6)} %compare.3, pred[]{:T(512)S(6)} %and.43, f32[256,3072]{1,0:T(8,128)} %copy-done.1), kind=kOutput, calls=%fused_computation.27.clone.1 | convolution fusion | flops 1222115328 | bytes 22413314 | tf_op jit(solution)/shard_map/while/body/eval_jaxpr/dot_general | solution.py:18
  743.8 10.9 %select_add_fusion.5 = f32[3072,768]{1,0:T(8,128)} fusion(f32[3072,768]{1,0:T(8,128)} %get-tuple-element.762, bf16[256,768]{1,0:T(8,128)(2,1)S(1)} %bitcast_select_fusion.12, pred[]{:T(512)S(6)} %compare.3, pred[]{:T(512)S(6)} %and.43, f32[256,3072]{1,0:T(8,128)} %copy-done.1), kind=kOutput, calls=%fused_computation.27.clone.1 | convolution fusion | flops 1222115328 | bytes 22413314 | tf_op jit(solution)/shard_map/while/body/eval_jaxpr/dot_general | solution.py:18
  762.1 152.2 %all-reduce.3.cloned.1.call-done = (bf16[8,256,768]{2,1,0:T(8,128)(2,1)}, bf16[8,256,768]{2,1,0:T(8,128)(2,1)}) async-done(((bf16[8,256,768]{2,1,0:T(8,128)(2,1)}, bf16[8,256,768]{2,1,0:T(8,128)(2,1)}), (bf16[8,256,768]{2,1,0:T(8,128)(2,1)}, bf16[8,256,768]{2,1,0:T(8,128)(2,1)})) %all-reduce.3.cloned.1.call-update) | async-done | bytes 6291472 | tf_op jit(solution)/shard_map/psum | solution.py:82
  (525 shorter events, 390.5 us)
Async XLA Ops:
  7.2 907.1 %all-reduce.3.cloned.1.call-start = ((), (), s32[]{:S(2)}) async-start(), calls=%async_computation | async-start | bytes 12582912 | tf_op jit(solution)/shard_map/psum | solution.py:82
  17.8 6.1 collective-permute-start
  33.4 9.3 collective-permute-start
  52.2 9.1 collective-permute-start
  70.7 9.1 collective-permute-start
  89.3 9.1 collective-permute-start
  107.9 9.1 collective-permute-start
  126.4 9.1 collective-permute-start
  145.0 9.1 collective-permute-start
  163.6 9.1 collective-permute-start
  182.1 9.1 collective-permute-start
  200.7 9.1 collective-permute-start
  219.3 9.1 collective-permute-start
  237.8 9.1 collective-permute-start
  256.4 9.1 collective-permute-start
  275.0 9.1 collective-permute-start
  297.5 11.9 %slice-start = ((s8[9437184]{0:T(1024)(128)(4,1)}), s8[1048576]{0:T(1024)(128)(4,1)S(1)}, s32[]{:S(2)}) async-start(s8[9437184]{0:T(1024)(128)(4,1)} %bitcast.119), calls=%async_computation.1 | async-start | bytes 2097152 | tf_op jit(solution)/shard_map/while
  299.9 13.2 %collective-permute-start.1 = (bf16[256,768]{1,0:T(8,128)(2,1)}, bf16[256,768]{1,0:T(8,128)(2,1)S(1)}, u32[]{:S(2)}, u32[]{:S(2)}) collective-permute-start(bf16[256,768]{1,0:T(8,128)(2,1)} %get-tuple-element.698), channel_id=1, source_target_pairs={{1,0},{2,1},{3,2},{4,3},{5,4},{6,5},{7,6},{9,8},{10,9},{11,10},{12... | collective-permute-start | bytes 1179656 | tf_op jit(solution)/shard_map/while/body/eval_jaxpr/ppermute | solution.py:76
  326.6 14.6 %slice-start = ((s8[9437184]{0:T(1024)(128)(4,1)}), s8[1048576]{0:T(1024)(128)(4,1)S(1)}, s32[]{:S(2)}) async-start(s8[9437184]{0:T(1024)(128)(4,1)} %bitcast.119), calls=%async_computation.1 | async-start | bytes 2097152 | tf_op jit(solution)/shard_map/while
  329.0 15.9 %collective-permute-start.1 = (bf16[256,768]{1,0:T(8,128)(2,1)}, bf16[256,768]{1,0:T(8,128)(2,1)S(1)}, u32[]{:S(2)}, u32[]{:S(2)}) collective-permute-start(bf16[256,768]{1,0:T(8,128)(2,1)} %get-tuple-element.698), channel_id=1, source_target_pairs={{1,0},{2,1},{3,2},{4,3},{5,4},{6,5},{7,6},{9,8},{10,9},{11,10},{12... | collective-permute-start | bytes 1179656 | tf_op jit(solution)/shard_map/while/body/eval_jaxpr/ppermute | solution.py:76
  330.3 10.9 %slice-start.1 = ((s8[9437184]{0:T(1024)(128)(4,1)}), s8[4194304]{0:T(1024)(128)(4,1)S(1)}, s32[]{:S(2)}) async-start(s8[9437184]{0:T(1024)(128)(4,1)} %bitcast.119), calls=%async_computation.2 | async-start | bytes 8388608 | tf_op jit(solution)/shard_map/while
  358.4 14.6 %slice-start = ((s8[9437184]{0:T(1024)(128)(4,1)}), s8[1048576]{0:T(1024)(128)(4,1)S(1)}, s32[]{:S(2)}) async-start(s8[9437184]{0:T(1024)(128)(4,1)} %bitcast.119), calls=%async_computation.1 | async-start | bytes 2097152 | tf_op jit(solution)/shard_map/while
  360.8 15.9 %collective-permute-start.1 = (bf16[256,768]{1,0:T(8,128)(2,1)}, bf16[256,768]{1,0:T(8,128)(2,1)S(1)}, u32[]{:S(2)}, u32[]{:S(2)}) collective-permute-start(bf16[256,768]{1,0:T(8,128)(2,1)} %get-tuple-element.698), channel_id=1, source_target_pairs={{1,0},{2,1},{3,2},{4,3},{5,4},{6,5},{7,6},{9,8},{10,9},{11,10},{12... | collective-permute-start | bytes 1179656 | tf_op jit(solution)/shard_map/while/body/eval_jaxpr/ppermute | solution.py:76
  362.1 10.9 %slice-start.1 = ((s8[9437184]{0:T(1024)(128)(4,1)}), s8[4194304]{0:T(1024)(128)(4,1)S(1)}, s32[]{:S(2)}) async-start(s8[9437184]{0:T(1024)(128)(4,1)} %bitcast.119), calls=%async_computation.2 | async-start | bytes 8388608 | tf_op jit(solution)/shard_map/while
  390.2 14.6 %slice-start = ((s8[9437184]{0:T(1024)(128)(4,1)}), s8[1048576]{0:T(1024)(128)(4,1)S(1)}, s32[]{:S(2)}) async-start(s8[9437184]{0:T(1024)(128)(4,1)} %bitcast.119), calls=%async_computation.1 | async-start | bytes 2097152 | tf_op jit(solution)/shard_map/while
  392.6 15.9 %collective-permute-start.1 = (bf16[256,768]{1,0:T(8,128)(2,1)}, bf16[256,768]{1,0:T(8,128)(2,1)S(1)}, u32[]{:S(2)}, u32[]{:S(2)}) collective-permute-start(bf16[256,768]{1,0:T(8,128)(2,1)} %get-tuple-element.698), channel_id=1, source_target_pairs={{1,0},{2,1},{3,2},{4,3},{5,4},{6,5},{7,6},{9,8},{10,9},{11,10},{12... | collective-permute-start | bytes 1179656 | tf_op jit(solution)/shard_map/while/body/eval_jaxpr/ppermute | solution.py:76
  422.0 14.6 %slice-start = ((s8[9437184]{0:T(1024)(128)(4,1)}), s8[1048576]{0:T(1024)(128)(4,1)S(1)}, s32[]{:S(2)}) async-start(s8[9437184]{0:T(1024)(128)(4,1)} %bitcast.119), calls=%async_computation.1 | async-start | bytes 2097152 | tf_op jit(solution)/shard_map/while
  424.4 15.9 %collective-permute-start.1 = (bf16[256,768]{1,0:T(8,128)(2,1)}, bf16[256,768]{1,0:T(8,128)(2,1)S(1)}, u32[]{:S(2)}, u32[]{:S(2)}) collective-permute-start(bf16[256,768]{1,0:T(8,128)(2,1)} %get-tuple-element.698), channel_id=1, source_target_pairs={{1,0},{2,1},{3,2},{4,3},{5,4},{6,5},{7,6},{9,8},{10,9},{11,10},{12... | collective-permute-start | bytes 1179656 | tf_op jit(solution)/shard_map/while/body/eval_jaxpr/ppermute | solution.py:76
  453.9 14.6 %slice-start = ((s8[9437184]{0:T(1024)(128)(4,1)}), s8[1048576]{0:T(1024)(128)(4,1)S(1)}, s32[]{:S(2)}) async-start(s8[9437184]{0:T(1024)(128)(4,1)} %bitcast.119), calls=%async_computation.1 | async-start | bytes 2097152 | tf_op jit(solution)/shard_map/while
  456.3 15.9 %collective-permute-start.1 = (bf16[256,768]{1,0:T(8,128)(2,1)}, bf16[256,768]{1,0:T(8,128)(2,1)S(1)}, u32[]{:S(2)}, u32[]{:S(2)}) collective-permute-start(bf16[256,768]{1,0:T(8,128)(2,1)} %get-tuple-element.698), channel_id=1, source_target_pairs={{1,0},{2,1},{3,2},{4,3},{5,4},{6,5},{7,6},{9,8},{10,9},{11,10},{12... | collective-permute-start | bytes 1179656 | tf_op jit(solution)/shard_map/while/body/eval_jaxpr/ppermute | solution.py:76
  485.7 14.6 %slice-start = ((s8[9437184]{0:T(1024)(128)(4,1)}), s8[1048576]{0:T(1024)(128)(4,1)S(1)}, s32[]{:S(2)}) async-start(s8[9437184]{0:T(1024)(128)(4,1)} %bitcast.119), calls=%async_computation.1 | async-start | bytes 2097152 | tf_op jit(solution)/shard_map/while
  488.1 15.9 %collective-permute-start.1 = (bf16[256,768]{1,0:T(8,128)(2,1)}, bf16[256,768]{1,0:T(8,128)(2,1)S(1)}, u32[]{:S(2)}, u32[]{:S(2)}) collective-permute-start(bf16[256,768]{1,0:T(8,128)(2,1)} %get-tuple-element.698), channel_id=1, source_target_pairs={{1,0},{2,1},{3,2},{4,3},{5,4},{6,5},{7,6},{9,8},{10,9},{11,10},{12... | collective-permute-start | bytes 1179656 | tf_op jit(solution)/shard_map/while/body/eval_jaxpr/ppermute | solution.py:76
  517.5 14.6 %slice-start = ((s8[9437184]{0:T(1024)(128)(4,1)}), s8[1048576]{0:T(1024)(128)(4,1)S(1)}, s32[]{:S(2)}) async-start(s8[9437184]{0:T(1024)(128)(4,1)} %bitcast.119), calls=%async_computation.1 | async-start | bytes 2097152 | tf_op jit(solution)/shard_map/while
  519.9 15.9 %collective-permute-start.1 = (bf16[256,768]{1,0:T(8,128)(2,1)}, bf16[256,768]{1,0:T(8,128)(2,1)S(1)}, u32[]{:S(2)}, u32[]{:S(2)}) collective-permute-start(bf16[256,768]{1,0:T(8,128)(2,1)} %get-tuple-element.698), channel_id=1, source_target_pairs={{1,0},{2,1},{3,2},{4,3},{5,4},{6,5},{7,6},{9,8},{10,9},{11,10},{12... | collective-permute-start | bytes 1179656 | tf_op jit(solution)/shard_map/while/body/eval_jaxpr/ppermute | solution.py:76
  549.3 14.6 %slice-start = ((s8[9437184]{0:T(1024)(128)(4,1)}), s8[1048576]{0:T(1024)(128)(4,1)S(1)}, s32[]{:S(2)}) async-start(s8[9437184]{0:T(1024)(128)(4,1)} %bitcast.119), calls=%async_computation.1 | async-start | bytes 2097152 | tf_op jit(solution)/shard_map/while
  551.7 15.9 %collective-permute-start.1 = (bf16[256,768]{1,0:T(8,128)(2,1)}, bf16[256,768]{1,0:T(8,128)(2,1)S(1)}, u32[]{:S(2)}, u32[]{:S(2)}) collective-permute-start(bf16[256,768]{1,0:T(8,128)(2,1)} %get-tuple-element.698), channel_id=1, source_target_pairs={{1,0},{2,1},{3,2},{4,3},{5,4},{6,5},{7,6},{9,8},{10,9},{11,10},{12... | collective-permute-start | bytes 1179656 | tf_op jit(solution)/shard_map/while/body/eval_jaxpr/ppermute | solution.py:76
  581.1 14.6 %slice-start = ((s8[9437184]{0:T(1024)(128)(4,1)}), s8[1048576]{0:T(1024)(128)(4,1)S(1)}, s32[]{:S(2)}) async-start(s8[9437184]{0:T(1024)(128)(4,1)} %bitcast.119), calls=%async_computation.1 | async-start | bytes 2097152 | tf_op jit(solution)/shard_map/while
  583.5 15.9 %collective-permute-start.1 = (bf16[256,768]{1,0:T(8,128)(2,1)}, bf16[256,768]{1,0:T(8,128)(2,1)S(1)}, u32[]{:S(2)}, u32[]{:S(2)}) collective-permute-start(bf16[256,768]{1,0:T(8,128)(2,1)} %get-tuple-element.698), channel_id=1, source_target_pairs={{1,0},{2,1},{3,2},{4,3},{5,4},{6,5},{7,6},{9,8},{10,9},{11,10},{12... | collective-permute-start | bytes 1179656 | tf_op jit(solution)/shard_map/while/body/eval_jaxpr/ppermute | solution.py:76
  612.9 14.6 %slice-start = ((s8[9437184]{0:T(1024)(128)(4,1)}), s8[1048576]{0:T(1024)(128)(4,1)S(1)}, s32[]{:S(2)}) async-start(s8[9437184]{0:T(1024)(128)(4,1)} %bitcast.119), calls=%async_computation.1 | async-start | bytes 2097152 | tf_op jit(solution)/shard_map/while
  615.3 15.9 %collective-permute-start.1 = (bf16[256,768]{1,0:T(8,128)(2,1)}, bf16[256,768]{1,0:T(8,128)(2,1)S(1)}, u32[]{:S(2)}, u32[]{:S(2)}) collective-permute-start(bf16[256,768]{1,0:T(8,128)(2,1)} %get-tuple-element.698), channel_id=1, source_target_pairs={{1,0},{2,1},{3,2},{4,3},{5,4},{6,5},{7,6},{9,8},{10,9},{11,10},{12... | collective-permute-start | bytes 1179656 | tf_op jit(solution)/shard_map/while/body/eval_jaxpr/ppermute | solution.py:76
  644.7 14.6 %slice-start = ((s8[9437184]{0:T(1024)(128)(4,1)}), s8[1048576]{0:T(1024)(128)(4,1)S(1)}, s32[]{:S(2)}) async-start(s8[9437184]{0:T(1024)(128)(4,1)} %bitcast.119), calls=%async_computation.1 | async-start | bytes 2097152 | tf_op jit(solution)/shard_map/while
  647.1 15.9 %collective-permute-start.1 = (bf16[256,768]{1,0:T(8,128)(2,1)}, bf16[256,768]{1,0:T(8,128)(2,1)S(1)}, u32[]{:S(2)}, u32[]{:S(2)}) collective-permute-start(bf16[256,768]{1,0:T(8,128)(2,1)} %get-tuple-element.698), channel_id=1, source_target_pairs={{1,0},{2,1},{3,2},{4,3},{5,4},{6,5},{7,6},{9,8},{10,9},{11,10},{12... | collective-permute-start | bytes 1179656 | tf_op jit(solution)/shard_map/while/body/eval_jaxpr/ppermute | solution.py:76
  676.5 14.6 %slice-start = ((s8[9437184]{0:T(1024)(128)(4,1)}), s8[1048576]{0:T(1024)(128)(4,1)S(1)}, s32[]{:S(2)}) async-start(s8[9437184]{0:T(1024)(128)(4,1)} %bitcast.119), calls=%async_computation.1 | async-start | bytes 2097152 | tf_op jit(solution)/shard_map/while
  678.9 15.9 %collective-permute-start.1 = (bf16[256,768]{1,0:T(8,128)(2,1)}, bf16[256,768]{1,0:T(8,128)(2,1)S(1)}, u32[]{:S(2)}, u32[]{:S(2)}) collective-permute-start(bf16[256,768]{1,0:T(8,128)(2,1)} %get-tuple-element.698), channel_id=1, source_target_pairs={{1,0},{2,1},{3,2},{4,3},{5,4},{6,5},{7,6},{9,8},{10,9},{11,10},{12... | collective-permute-start | bytes 1179656 | tf_op jit(solution)/shard_map/while/body/eval_jaxpr/ppermute | solution.py:76
  708.3 14.6 %slice-start = ((s8[9437184]{0:T(1024)(128)(4,1)}), s8[1048576]{0:T(1024)(128)(4,1)S(1)}, s32[]{:S(2)}) async-start(s8[9437184]{0:T(1024)(128)(4,1)} %bitcast.119), calls=%async_computation.1 | async-start | bytes 2097152 | tf_op jit(solution)/shard_map/while
  710.7 15.9 %collective-permute-start.1 = (bf16[256,768]{1,0:T(8,128)(2,1)}, bf16[256,768]{1,0:T(8,128)(2,1)S(1)}, u32[]{:S(2)}, u32[]{:S(2)}) collective-permute-start(bf16[256,768]{1,0:T(8,128)(2,1)} %get-tuple-element.698), channel_id=1, source_target_pairs={{1,0},{2,1},{3,2},{4,3},{5,4},{6,5},{7,6},{9,8},{10,9},{11,10},{12... | collective-permute-start | bytes 1179656 | tf_op jit(solution)/shard_map/while/body/eval_jaxpr/ppermute | solution.py:76
  740.1 14.6 %slice-start = ((s8[9437184]{0:T(1024)(128)(4,1)}), s8[1048576]{0:T(1024)(128)(4,1)S(1)}, s32[]{:S(2)}) async-start(s8[9437184]{0:T(1024)(128)(4,1)} %bitcast.119), calls=%async_computation.1 | async-start | bytes 2097152 | tf_op jit(solution)/shard_map/while
  742.5 15.9 %collective-permute-start.1 = (bf16[256,768]{1,0:T(8,128)(2,1)}, bf16[256,768]{1,0:T(8,128)(2,1)S(1)}, u32[]{:S(2)}, u32[]{:S(2)}) collective-permute-start(bf16[256,768]{1,0:T(8,128)(2,1)} %get-tuple-element.698), channel_id=1, source_target_pairs={{1,0},{2,1},{3,2},{4,3},{5,4},{6,5},{7,6},{9,8},{10,9},{11,10},{12... | collective-permute-start | bytes 1179656 | tf_op jit(solution)/shard_map/while/body/eval_jaxpr/ppermute | solution.py:76
  (120 other events, 728.4 us)
Sparse Core Ops, SparseCore 0:
  762.2 152.0 all-reduce.2
where the time goes:
time: 930 us; the launch traced here: 927 us
  matrix products  472 us (51%)
  waiting for transfers between devices  152 us (16%)
  local copies, waits for them, and re-layouts  126 us (14%)
  starting transfers between devices  109 us (12%)
  other arithmetic  50.6 us (5%)
  between operations  14.1 us (2%)
    dot_general x15, matrix products, _bwd_layer(): jnp.dot(u.astype(jnp.bfloat16).T, g, preferred_element_type=jnp.float32)  161 us
    psum x1, waiting for transfers between devices, body(): y = lax.psum(y, 'stage')  152 us
    dot_general x15, matrix products, _fwd_layer(): jnp.dot(u, w2, preferred_element_type=jnp.float32)  116 us
    ppermute x15, starting transfers between devices, fwd_tick(): recv = lax.ppermute(h, 'stage', fwd_perm)  89.6 us
    while x285, local copies, waits for them, and re-layouts  71.6 us
    dot_general x15, matrix products, _bwd_layer(): z = jnp.dot(h, w1, preferred_element_type=jnp.float32)  60.8 us
    dot_general x15, matrix products, _bwd_layer(): dw1 = jnp.dot(h.T, dz, preferred_element_type=jnp.float32)  54.5 us
    dynamic_slice x45, local copies, waits for them, and re-layouts, _put(): old = lax.dynamic_index_in_dim(buf, i, 0, keepdims=False)  44.4 us
  transfers between devices with their start and end apart: 31, of which 1 were waited for; matrix products, arithmetic and copies ran while one was open for 28% of the time, Pallas kernels for 0%

commit v1 on v0

v1 whole, which is shorter than its diff:
```python
import functools

import jax
import jax.numpy as jnp
from jax import lax
from jax.experimental import pallas as pl
from jax.experimental.pallas import tpu as pltpu
from jax.sharding import PartitionSpec as P

MESH = pl.DeviceIdType.MESH
f32 = jnp.float32
bf16 = jnp.bfloat16
D = 768
F = 3072
C = 128
G = 2
RING = 4
TN = 512
C0 = 0.7978845608028654
C1 = 0.044715

WORDS = (
    (0, 204734464, 338466073, 156340875, 422098187, 579749972, 1073727780),
    (5, 555745280, 560252185, 428163866, 591762210, 577115404, 1073726668),
    (5, 203423744, 338466073, 439456395, 422098185, 609339476, 1073727780),
    (5, 153092096, 208187987, 591763554, 176531553, 579650841, 1073727780),
    (5, 404885504, 338465825, 438973003, 422098185, 343033940, 1073727780),
    (5, 134578696, 153944601, 439399514, 608999585, 613501137, 1073727780),
    (17858565, 137105675, 142872644, 189022728, 613553825, 323832100, 1073718483),
    (137105477, 17043544, 17043521, 445452353, 443168026, 613565716, 1073727780),
)
STEPS = 10


def _dot(a, b):
    return jnp.dot(a, b, preferred_element_type=f32)


def _dot_t(a, b):
    return lax.dot_general(a, b, (((0,), (0,)), ((), ())), preferred_element_type=f32)


def _when(cond):
    return pl.when(cond)


def _pipeline(n_st, n_ch, x, g, w1h, w2h, y, dx, a1, a2, zh, uh, dh,
              w1, w2, w1t, w2t, hb, gb, zb, ub, db, uw, dw, fo, bo,
              wsem, hsem, gsem, ysem, xsem, fsem, bsem, osem, rsem, zwsem, zrsem, udsem, rdsem):
    d = lax.axis_index("data")
    s = lax.axis_index("stage")
    last = n_st - 1
    spill = s < n_st - 2
    even = s % 2 == 0

    def peer(k):
        return (d, k)

    loads = [pltpu.make_async_copy(w1h.at[0], w1, wsem.at[0]), pltpu.make_async_copy(w2h.at[0], w2, wsem.at[1])]
    for c in loads:
        c.start()

    @_when(s == 0)
    def _():
        def f(i, _):
            pltpu.make_async_copy(x.at[i], hb.at[i], hsem.at[i]).start()
            return 0
        lax.fori_loop(0, n_ch, f, 0)

    @_when(s == last)
    def _():
        def f(i, _):
            pltpu.make_async_copy(g.at[i], gb.at[i], gsem.at[i]).start()
            return 0
        lax.fori_loop(0, n_ch, f, 0)

    bar = pltpu.get_barrier_semaphore()
    for off in (-2, -1, 1, 2):
        @_when((s + off >= 0) & (s + off < n_st))
        def _(off=off):
            pl.semaphore_signal(bar, inc=1, device_id=peer(s + off), device_id_type=MESH)
    peers = jnp.minimum(s, 2) + jnp.minimum(last - s, 2)
    pl.semaphore_wait(bar, peers)

    for c in loads:
        c.wait()

    def send_f(i, r):
        return pltpu.make_async_remote_copy(src_ref=fo.at[r], dst_ref=hb.at[i], send_sem=fsem.at[r], recv_sem=hsem.at[i],
                                            device_id=peer(s + 1), device_id_type=MESH)

    def send_y(i, r):
        return pltpu.make_async_remote_copy(src_ref=fo.at[r], dst_ref=y.at[i], send_sem=fsem.at[r], recv_sem=ysem.at[i],
                                            device_id=peer(s - 1), device_id_type=MESH)

    def own_y(i, r):
        return pltpu.make_async_copy(fo.at[r], y.at[i], osem.at[r])

    def send_b(i, r):
        return pltpu.make_async_remote_copy(src_ref=bo.at[r], dst_ref=gb.at[i], send_sem=bsem.at[r], recv_sem=gsem.at[i],
                                            device_id=peer(s - 1), device_id_type=MESH)

    def send_x(i, r):
        return pltpu.make_async_remote_copy(src_ref=bo.at[r], dst_ref=dx.at[i], send_sem=bsem.at[r], recv_sem=xsem.at[i],
                                            device_id=peer(s + 1), device_id_type=MESH)

    def own_x(i, r):
        return pltpu.make_async_copy(bo.at[r], dx.at[i], osem.at[r])

    def relay(ref, i, sem, k, dev):
        return pltpu.make_async_remote_copy(src_ref=ref.at[i], dst_ref=ref.at[i], send_sem=rsem.at[k, i], recv_sem=sem.at[i],
                                            device_id=peer(dev), device_id_type=MESH)

    def write_z(i):
        return pltpu.make_async_copy(zb.at[i % 2], zh.at[i], zwsem.at[i % 2])

    def read_z(i):
        return pltpu.make_async_copy(zh.at[i], zb.at[2 + i % 2], zrsem.at[i % 2])

    def write_ud(i):
        rows = pl.ds(pl.multiple_of((i % G) * C, C), C)
        return (pltpu.make_async_copy(ub.at[i % 2], uh.at[i // G, rows], udsem.at[0, i % 2]),
                pltpu.make_async_copy(db.at[i % 2], dh.at[i // G, rows], udsem.at[1, i % 2]))

    def read_ud(k):
        return (pltpu.make_async_copy(uh.at[k], uw.at[k % 2], rdsem.at[0, k % 2]),
                pltpu.make_async_copy(dh.at[k], dw.at[k % 2], rdsem.at[1, k % 2]))

    def ensure_z(done, want):
        for j in range(2):
            @_when(done + j < want)
            def _(j=j):
                write_z(done + j).wait()

    def ensure_ud(done, want):
        for j in range(2):
            @_when(done + j < want)
            def _(j=j):
                for c in write_ud(done + j):
                    c.wait()

    def forward(i, zw):
        r = i % RING
        zs = jnp.where(spill, i % 2, i % 4)

        @_when(spill)
        def _():
            ensure_z(zw, i - 1)

        pltpu.make_async_copy(x.at[i], hb.at[i], hsem.at[i]).wait()

        @_when(i >= RING)
        def _():
            send_f(i, r).wait_send()

            @_when(s == last)
            def _():
                own_y(i, r).wait()

        h = hb[i]
        us = []
        for n in range(F // TN):
            sl = pl.ds(n * TN, TN)
            z = _dot(h, w1[:, sl])
            zb[zs, :, sl] = z
            t = jnp.tanh(z * (C0 + (C0 * C1) * (z * z)))
            us.append((z * (0.5 * (1.0 + t))).astype(bf16))
        u = jnp.concatenate(us, axis=1)
        fo[r] = (h.astype(f32) + _dot(u, w2[...])).astype(bf16)

        @_when(s < last)
        def _():
            send_f(i, r).start()

        @_when(s == last)
        def _():
            send_y(i, r).start()
            own_y(i, r).start()

        @_when(spill)
        def _():
            write_z(i).start()

            @_when(i == 4)
            def _():
                read_z(0).start()

    def backward(i, zw, ud):
        r = i % RING
        zs = jnp.where(spill, 2 + i % 2, i % 4)

        @_when(spill)
        def _():
            read_z(i).wait()
            ensure_z(zw, jnp.minimum(i + 2, n_ch))

            @_when(i + 1 < n_ch)
            def _():
                read_z(i + 1).start()

        ensure_ud(ud, i - 1)
        pltpu.make_async_copy(g.at[i], gb.at[i], gsem.at[i]).wait()

        @_when(i >= RING)
        def _():
            send_b(i, r).wait_send()

            @_when(s == 0)
            def _():
                own_x(i, r).wait()

        gg = gb[i]
        q = i % 2
        for n in range(F // TN):
            sl = pl.ds(n * TN, TN)
            du = _dot(gg, w2t[:, sl])
            z = zb[zs, :, sl]
            z2 = z * z
            t = jnp.tanh(z * (C0 + (C0 * C1) * z2))
            p = 0.5 * (1.0 + t)
            ub[q, :, sl] = (z * p).astype(bf16)
            dg = p + ((0.5 * z) * (1.0 - t * t)) * (C0 + (3.0 * C0 * C1) * z2)
            db[q, :, sl] = (dg * du).astype(bf16)
        bo[r] = (gg.astype(f32) + _dot(db[q], w1t[...])).astype(bf16)

        @_when(s > 0)
        def _():
            send_b(i, r).start()

        @_when(s == 0)
        def _():
            send_x(i, r).start()
            own_x(i, r).start()

        for c in write_ud(i):
            c.start()

    def prefetch(k, ud):
        ensure_ud(ud, G * (k + 1))
        for c in read_ud(k):
            c.start()

    def weights(k):
        for c in read_ud(k):
            c.wait()
        q = k % 2
        rows = pl.ds(G * k, G)
        h = hb[rows].reshape(G * C, D)
        gg = gb[rows].reshape(G * C, D)
        for n in range(F // TN):
            sl = pl.ds(n * TN, TN)
            a1[:, sl] += _dot_t(h, dw[q, :, sl])
        for n in range(F // TN):
            sl = pl.ds(n * TN, TN)
            a2[sl, :] += _dot_t(uw[q, :, sl], gg)

    def relay_step(i):
        @_when(even)
        def _():
            pltpu.make_async_copy(y.at[i], y.at[i], ysem.at[i]).wait()

            @_when(s < n_st - 2)
            def _():
                relay(y, i, ysem, 0, s + 1).start()

            @_when(s >= 2)
            def _():
                relay(y, i, ysem, 1, s - 2).start()

        @_when(jnp.logical_not(even))
        def _():
            pltpu.make_async_copy(dx.at[i], dx.at[i], xsem.at[i]).wait()

            @_when(s > 1)
            def _():
                relay(dx, i, xsem, 0, s - 1).start()

            @_when(s < last)
            def _():
                relay(dx, i, xsem, 1, s + 2).start()

    def transposes():
        def f(n, _):
            sl = pl.ds(pl.multiple_of(n * 256, 256), 256)
            w1t[sl, :] = w1[:, sl].T
            w2t[:, sl] = w2[sl, :].T
            a1[:, sl] = jnp.zeros((D, 256), f32)
            a2[sl, :] = jnp.zeros((256, D), f32)
            return 0
        lax.fori_loop(0, F // 256, f, 0)

    def step(j, carry):
        word, nf, nb, nw, npf, nr, zw, ud = carry
        op = word % 8
        is_f, is_b, is_p = op == 0, op == 1, op == 3

        @_when(is_f)
        def _():
            forward(nf, zw)

        @_when(is_b)
        def _():
            backward(nb, zw, ud)

        @_when(op == 2)
        def _():
            weights(nw)

        @_when(is_p)
        def _():
            prefetch(npf, ud)

        @_when(op == 4)
        def _():
            relay_step(nr)

        @_when(op == 5)
        def _():
            transposes()

        zw = jnp.where(is_f, jnp.maximum(zw, nf - 1), zw)
        zw = jnp.where(is_b, jnp.maximum(zw, jnp.minimum(nb + 2, n_ch)), zw)
        ud = jnp.where(is_b, jnp.maximum(ud, nb - 1), ud)
        ud = jnp.where(is_p, jnp.maximum(ud, G * (npf + 1)), ud)
        one = lambda k: jnp.where(op == k, 1, 0)
        return (word // 8, nf + one(0), nb + one(1), nw + one(2), npf + one(3), nr + one(4), zw, ud)

    zero = s * 0
    state = (zero,) * 7
    for k in range(len(WORDS[0])):
        word = zero
        for q in range(n_st):
            word = jnp.where(s == q, WORDS[q][k], word)
        if k == 0:
            words = [word]
        else:
            words.append(word)

    def block(k, carry):
        word = words[0]
        for q in range(1, len(words)):
            word = jnp.where(k == q, words[q], word)
        out = lax.fori_loop(0, STEPS, step, (word, *carry))
        return out[1:]

    lax.fori_loop(0, len(words), block, state)

    for j in range(RING):
        i = n_ch - RING + j
        r = i % RING
        send_f(i, r).wait_send()
        send_b(i, r).wait_send()

        @_when(s == last)
        def _(i=i, r=r):
            own_y(i, r).wait()

        @_when(s == 0)
        def _(i=i, r=r):
            own_x(i, r).wait()

    def finish(i, _):
        @_when(even)
        def _():
            @_when(s < n_st - 2)
            def _():
                relay(y, i, ysem, 0, s + 1).wait_send()

            @_when(s >= 2)
            def _():
                relay(y, i, ysem, 1, s - 2).wait_send()

            @_when(s > 0)
            def _():
                pltpu.make_async_copy(dx.at[i], dx.at[i], xsem.at[i]).wait()

        @_when(jnp.logical_not(even))
        def _():
            @_when(s > 1)
            def _():
                relay(dx, i, xsem, 0, s - 1).wait_send()

            @_when(s < last)
            def _():
                relay(dx, i, xsem, 1, s + 2).wait_send()
                pltpu.make_async_copy(y.at[i], y.at[i], ysem.at[i]).wait()
        return 0
    lax.fori_loop(0, n_ch, finish, 0)


def _write_out(n_ch, y, dx, a1, a2, yo, dxo, d1, d2, yb, xb, sem_w, sem_r, sem_o):
    parts = 4
    big = []
    for p in range(parts):
        r1 = pl.ds(p * (D // parts), D // parts)
        r2 = pl.ds(p * (F // parts), F // parts)
        big.append(pltpu.make_async_copy(a1.at[r1], d1.at[0, r1], sem_w.at[0, p]))
        big.append(pltpu.make_async_copy(a2.at[r2], d2.at[0, r2], sem_w.at[1, p]))
    ins = [pltpu.make_async_copy(y, yb, sem_r.at[0]), pltpu.make_async_copy(dx, xb, sem_r.at[1])]
    outs = [pltpu.make_async_copy(yb, yo, sem_o.at[0]), pltpu.make_async_copy(xb, dxo, sem_o.at[1])]
    for c in ins:
        c.start()
    for c in big:
        c.start()
    for c, o in zip(ins, outs):
        c.wait()
        o.start()
    for c in big:
        c.wait()
    for o in outs:
        o.wait()


def solution(mesh):
    n_st = mesh.shape["stage"]

    def body(x, g, w1, w2):
        n_mb, rows, _ = x.shape
        n_ch = n_mb * rows // C
        xc = x.reshape(n_ch, C, D)
        gc = g.reshape(n_ch, C, D)
        hbm = pl.BlockSpec(memory_space=pltpu.HBM)
        vmem = pl.BlockSpec(memory_space=pltpu.VMEM)
        dma = pltpu.SemaphoreType.DMA
        chunk = (n_ch, C, D)
        y, dx, a1, a2, _, _, _ = pl.pallas_call(
            functools.partial(_pipeline, n_st, n_ch),
            out_shape=[pltpu.HBM(chunk, bf16), pltpu.HBM(chunk, bf16), pltpu.VMEM((D, F), f32), pltpu.VMEM((F, D), f32),
                       pltpu.HBM((n_ch, C, F), f32), pltpu.HBM((n_ch // G, G * C, F), bf16), pltpu.HBM((n_ch // G, G * C, F), bf16)],
            in_specs=[hbm] * 4,
            out_specs=[hbm, hbm, vmem, vmem, hbm, hbm, hbm],
            scratch_shapes=[
                pltpu.VMEM((D, F), bf16), pltpu.VMEM((F, D), bf16), pltpu.VMEM((F, D), bf16), pltpu.VMEM((D, F), bf16),
                pltpu.VMEM(chunk, bf16), pltpu.VMEM(chunk, bf16), pltpu.VMEM((4, C, F), f32),
                pltpu.VMEM((2, C, F), bf16), pltpu.VMEM((2, C, F), bf16),
                pltpu.VMEM((2, G * C, F), bf16), pltpu.VMEM((2, G * C, F), bf16),
                pltpu.VMEM((RING, C, D), bf16), pltpu.VMEM((RING, C, D), bf16),
                dma((2,)), dma((n_ch,)), dma((n_ch,)), dma((n_ch,)), dma((n_ch,)), dma((RING,)), dma((RING,)), dma((RING,)),
                dma((2, n_ch)), dma((2,)), dma((2,)), dma((2, 2)), dma((2, 2)),
            ],
            compiler_params=pltpu.CompilerParams(collective_id=0, has_side_effects=True, vmem_limit_bytes=46_000_000),
            name="pipeline",
        )(xc, gc, w1, w2)
        y, dx, d1, d2 = pl.pallas_call(
            functools.partial(_write_out, n_ch),
            out_shape=[pltpu.HBM(chunk, bf16), pltpu.HBM(chunk, bf16), pltpu.HBM((1, D, F), f32), pltpu.HBM((1, F, D), f32)],
            in_specs=[hbm, hbm, vmem, vmem],
            out_specs=[hbm] * 4,
            scratch_shapes=[pltpu.VMEM(chunk, bf16), pltpu.VMEM(chunk, bf16), dma((2, 4)), dma((2,)), dma((2,))],
            compiler_params=pltpu.CompilerParams(has_side_effects=True, vmem_limit_bytes=7_000_000),
            name="write_out",
        )(*(pltpu.with_memory_space_constraint(v, pltpu.HBM) for v in (y, dx)), a1, a2)
        return y.reshape(x.shape), dx.reshape(x.shape), d1, d2

    return jax.shard_map(body, mesh=mesh,
                         in_specs=(P("data"), P("data"), P("stage"), P("stage")),
                         out_specs=(P("data"), P("data"), P(("data", "stage")), P(("data", "stage"))),
                         check_vma=False)
```

time: 930 us -> 163 us (0.18)
  matrix products: 472 us -> 0 us
  Pallas kernels: 0 us -> 162 us
  waiting for transfers between devices: 152 us -> 0 us
  local copies, waits for them, and re-layouts: 126 us -> 0 us
  starting transfers between devices: 109 us -> 0 us
  other arithmetic: 50.6 us -> 0 us
  between operations: 14.1 us -> 0.64 us
    dot_general x90 -> x0, matrix products: 472 us -> none  [the longest x15 161 us: _bwd_layer(): jnp.dot(u.astype(jnp.bfloat16).T, g, preferred_element_type=jnp.float32)]
    pallas_call x0 -> x2, Pallas kernels: none -> 162 us  [the longest x1 152 us: body(): pl.pallas_call(functools.partial(_pipeline, n_st, n_ch), out_shape=[pltpu...]
    psum x1 -> x0, waiting for transfers between devices: 152 us -> none  [body(): y = lax.psum(y, 'stage')]
    ppermute x30 -> x0, starting transfers between devices: 109 us -> none  [the longest x15 89.6 us: fwd_tick(): recv = lax.ppermute(h, 'stage', fwd_perm)]
    while x285 -> x0, local copies, waits for them, and re-layouts: 71.6 us -> none
    dynamic_slice x45 -> x0, local copies, waits for them, and re-layouts: 44.4 us -> none  [_put(): old = lax.dynamic_index_in_dim(buf, i, 0, keepdims=False)]
    dynamic_update_slice x15 -> x0, other arithmetic: 28.4 us -> none  [_put(): return lax.dynamic_update_index_in_dim(buf, jnp.where(ok, val, old), i, 0)]
    select_n x15 -> x0, other arithmetic: 22.2 us -> none  [bwd_tick(): jnp.where(last, lax.dynamic_index_in_dim(g, mc, 0, keepdims=False), recv)]
  transfers between devices with their start and end apart: 31 -> 0, of which waited for: 1 -> 0; matrix products, arithmetic and copies ran while one was open for 28% -> 0% of each run, Pallas kernels for 0% -> 0%
where the time goes in v1:
time: 163 us; the launch traced here: 162 us
  Pallas kernels  162 us (99%)
    pallas_call x1, Pallas kernels, body(): pl.pallas_call(functools.partial(_pipeline, n_st, n_ch), out_shape=[pltpu...  152 us
    pallas_call x1, Pallas kernels, body(): pl.pallas_call(functools.partial(_write_out, n_ch), out_shape=[pltpu.HBM(...  10.1 us

profile of v1, /device:TPU:0, one launch (start us, length us, event | category | flops | bytes accessed | tf_op | source)
XLA Modules:
  0.0 162.4 jit_solution(2048344311666020887)
XLA Ops:
  0.6 151.7 %pipeline.1 = (bf16[16,128,768]{2,1,0:T(8,128)(2,1)}, bf16[16,128,768]{2,1,0:T(8,128)(2,1)}, f32[768,3072]{1,0:T(8,128)S(1)}, f32[3072,768]{1,0:T(8,128)S(1)}, f...) custom-call(bf16[16,128,768]{2,1,0:T(8,128)(2,1)} %bitcast.4, ...), custom_call_target="tpu_custom_call" | custom-call | tf_op jit(solution)/shard_map/pipeline/pallas_call | solution.py:426
  152.3 10.1 %write_out.1 = (bf16[16,128,768]{2,1,0:T(8,128)(2,1)}, bf16[16,128,768]{2,1,0:T(8,128)(2,1)}, f32[1,768,3072]{2,1,0:T(8,128)}, f32[1,3072,768]{2,1,0:T(8,128)}) custom-call(bf16[16,128,768]{2,1,0:T(8,128)(2,1)} %get-tuple-element.12.y, bf16[16,128,768]{2,1,0:T(8,128)(2,1)} %get-tuple-element.13.dx, f32[768,3072]{1,0:T(8,128)S(1)} %get-tuple-element.14.a1, ...), custom_call_target="tpu_custom_call" | custom-call | tf_op jit(solution)/shard_map/write_out/pallas_call | solution.py:444

commit v2 on v1

v2 whole, which is shorter than its diff:
```python
import functools

import jax
import jax.numpy as jnp
from jax import lax
from jax.experimental import pallas as pl
from jax.experimental.pallas import tpu as pltpu
from jax.sharding import PartitionSpec as P

MESH = pl.DeviceIdType.MESH
f32 = jnp.float32
bf16 = jnp.bfloat16
D = 768
F = 3072
C = 128
H = 64
RING = 4
TN = 256
TW = 512
C0 = 0.7978845608028654
C1 = 0.044715

WORDS = (
    (0, 614465536, 472959076, 439399505, 294228753, 208181387, 592582754, 344601890, 613558548, 1073741820),
    (0, 564133888, 210286857, 439490842, 589710436, 210585684, 189928226, 344246436, 307341587, 1073741818),
    (5, 603996160, 193337440, 591705186, 438965897, 560600140, 592595018, 344601890, 613558548, 1073741820),
    (5, 134479872, 157853785, 610834644, 208279825, 592495884, 338827425, 340895907, 613558548, 1073741820),
    (67108869, 142612736, 539771396, 157849809, 156284002, 591799066, 445270281, 579971236, 613500194, 1073741820),
    (16777221, 23101504, 555778753, 562370186, 444999770, 445257996, 445265172, 609305876, 613566756, 1073741820),
    (75501829, 540115713, 201595073, 25215041, 205914657, 613566554, 613566756, 308884644, 307046035, 1073741818),
    (184815685, 17045000, 17043521, 293634572, 579683540, 344802586, 342501588, 613500180, 613566756, 1073741820),
)
STEPS = 10


def _dot(a, b):
    return jnp.dot(a, b, preferred_element_type=f32)


def _dot_t(a, b):
    return lax.dot_general(a, b, (((0,), (0,)), ((), ())), preferred_element_type=f32)


def _gelu(z):
    q = (C0 * C1) * (z * z)
    p = 0.5 * jnp.tanh(z * (C0 + q)) + 0.5
    u = z * p
    return u.astype(bf16), p + (u * (1.0 - p)) * (2.0 * C0 + 6.0 * q)


def _pipeline(n_st, n_ch, x, g, w1h, w2h, lf, rb, a1, a2, zh, uh, dh,
              w1, w2, w1t, w2t, hb, gb, zb, ub, db, uw, dw, fo, bo,
              wsem, hsem, gsem, psem, lsem, fsem, bsem, osem, rsem, zwsem, zrsem, uwsem, dwsem, ursem, drsem):
    d = lax.axis_index("data")
    s = lax.axis_index("stage")
    last = n_st - 1
    end = n_ch - 1
    pieces = 2 * end
    spill = s < n_st - 2
    even = s % 2 == 0
    top, low = pl.ds(0, H), pl.ds(H, H)

    def peer(k):
        return (d, k)

    def sized(i, small, full):
        short = (i == 0) | (i == end)
        pl.when(short)(small)
        pl.when(jnp.logical_not(short))(full)

    def row(i):
        return jnp.maximum(i * C - H, 0)

    def load(src, dst, sem, i, rows):
        at = pl.ds(pl.multiple_of(row(i), H), rows)
        return pltpu.make_async_copy(src.at[at], dst.at[i, pl.ds(0, rows)], sem.at[i])

    def landed(buf, sem, i):
        def wait(rows):
            part = buf.at[i, pl.ds(0, rows)]
            pltpu.make_async_copy(part, part, sem.at[i]).wait()
        sized(i, lambda: wait(H), lambda: wait(C))

    loads = [pltpu.make_async_copy(w1h.at[0], w1, wsem.at[0]), pltpu.make_async_copy(w2h.at[0], w2, wsem.at[1])]

    def load_all(src, dst, sem):
        def f(i, _):
            sized(i, lambda: load(src, dst, sem, i, H).start(), lambda: load(src, dst, sem, i, C).start())
            return 0
        return f

    @pl.when(s == 0)
    def _():
        load(x, hb, hsem, 0, H).start()

    for c in loads:
        c.start()

    @pl.when(s == 0)
    def _():
        lax.fori_loop(1, n_ch, load_all(x, hb, hsem), 0)

    @pl.when(s == last)
    def _():
        lax.fori_loop(0, n_ch, load_all(g, gb, gsem), 0)

    hb[0, low, :] = jnp.zeros((H, D), bf16)
    gb[0, low, :] = jnp.zeros((H, D), bf16)

    bar = pltpu.get_barrier_semaphore()
    near = (-2, -1, 1, 2)
    for off in near:
        @pl.when((s + off >= 0) & (s + off < n_st))
        def _(off=off):
            pl.semaphore_signal(bar, inc=1, device_id=peer(s + off), device_id_type=MESH)
    for k in range(3, n_st, 2):
        @pl.when(s == 0)
        def _(k=k):
            pl.semaphore_signal(bar, inc=1, device_id=peer(k), device_id_type=MESH)

        @pl.when(s == k)
        def _(k=k):
            pl.semaphore_signal(bar, inc=1, device_id=peer(0), device_id_type=MESH)
    far = jnp.where(s == 0, (n_st - 2) // 2, jnp.where((s % 2 == 1) & (s >= 3), 1, 0))
    pl.semaphore_wait(bar, jnp.minimum(s, 2) + jnp.minimum(last - s, 2) + far)

    for c in loads:
        c.wait()

    def send(src, r, dst, i, ssem, rsem_, dev, rows):
        return pltpu.make_async_remote_copy(src_ref=src.at[r, pl.ds(0, rows)], dst_ref=dst.at[i, pl.ds(0, rows)],
                                            send_sem=ssem.at[0, r], recv_sem=rsem_.at[i], device_id=peer(dev), device_id_type=MESH)

    def send_f(i, r, rows):
        return send(fo, r, hb, i, fsem, hsem, s + 1, rows)

    def send_b(i, r, rows):
        return send(bo, r, gb, i, bsem, gsem, s - 1, rows)

    def first_piece(i):
        return jnp.maximum(2 * i - 1, 0)

    def hand(src, r, k, p, ssem, dev):
        return pltpu.make_async_remote_copy(src_ref=src.at[r, pl.ds(k * H, H)], dst_ref=rb.at[p], send_sem=ssem.at[k, r],
                                            recv_sem=psem.at[p], device_id=peer(dev), device_id_type=MESH)

    def keep(src, r, k, p):
        return pltpu.make_async_copy(src.at[r, pl.ds(k * H, H)], lf.at[p], osem.at[k, r])

    def out_start(src, r, i, ssem, dev):
        p = first_piece(i)
        hand(src, r, 0, p, ssem, dev).start()
        keep(src, r, 0, p).start()

        def more():
            hand(src, r, 1, p + 1, ssem, dev).start()
            keep(src, r, 1, p + 1).start()
        sized(i, lambda: None, more)

    def out_wait(src, r, i, ssem, dev):
        p = first_piece(i)
        hand(src, r, 0, p, ssem, dev).wait_send()
        keep(src, r, 0, p).wait()

        def more():
            hand(src, r, 1, p + 1, ssem, dev).wait_send()
            keep(src, r, 1, p + 1).wait()
        sized(i, lambda: None, more)

    def direct(r, k):
        return pltpu.make_async_remote_copy(src_ref=bo.at[r, top], dst_ref=rb.at[pieces - 1], send_sem=lsem.at[0, k],
                                            recv_sem=psem.at[pieces - 1], device_id=peer(k), device_id_type=MESH)

    def onward(p, dev):
        return pltpu.make_async_remote_copy(src_ref=rb.at[p], dst_ref=rb.at[p], send_sem=rsem.at[0, p], recv_sem=psem.at[p],
                                            device_id=peer(dev), device_id_type=MESH)

    def across(p, dev):
        return pltpu.make_async_remote_copy(src_ref=rb.at[p], dst_ref=lf.at[p], send_sem=rsem.at[1, p], recv_sem=lsem.at[1, p],
                                            device_id=peer(dev), device_id_type=MESH)

    def write_z(i):
        return pltpu.make_async_copy(zb.at[i % 2], zh.at[i], zwsem.at[i % 2])

    def read_z(i):
        return pltpu.make_async_copy(zh.at[i], zb.at[2 + i % 2], zrsem.at[i % 2])

    def group_rows(i):
        return (i - 1) // 2, pl.ds(pl.multiple_of(((i - 1) % 2) * C, C), C)

    def write_u(i):
        k, rows = group_rows(i)
        return pltpu.make_async_copy(ub.at[i % 2], uh.at[k, rows], uwsem.at[i % 2])

    def write_d(i):
        k, rows = group_rows(i)
        return pltpu.make_async_copy(db.at[i % 2], dh.at[k, rows], dwsem.at[i % 2])

    def read_u(k):
        return pltpu.make_async_copy(uh.at[k], uw.at[k % 2], ursem.at[k % 2])

    def read_d(k):
        return pltpu.make_async_copy(dh.at[k], dw.at[k % 2], drsem.at[k % 2])

    def ensure(write, done, want, low_=0):
        for j in range(2):
            @pl.when((done + j < want) & (done + j >= low_))
            def _(j=j):
                write(done + j).wait()

    def forward(i, zw, uc):
        r = i % RING
        zs = jnp.where(spill, i % 2, i % 4)
        q = i % 2

        @pl.when(spill)
        def _():
            ensure(write_z, zw, i - 1)

        ensure(write_u, uc, i - 1, 1)
        landed(hb, hsem, i)

        @pl.when(i >= RING)
        def _():
            @pl.when(s < last)
            def _():
                sized(i - RING, lambda: send_f(i, r, H).wait_send(), lambda: send_f(i, r, C).wait_send())

            @pl.when(s == last)
            def _():
                out_wait(fo, r, i - RING, fsem, s - 1)

        @pl.when(i == 0)
        def _():
            hb[end, low, :] = hb[0, top, :]

        h = hb[i]
        for n in range(F // TN):
            sl = pl.ds(n * TN, TN)
            u, gp = _gelu(_dot(h, w1[:, sl]))
            zb[zs, :, sl] = gp
            ub[q, :, sl] = u
        acc = h.astype(f32)
        for n in range(F // TN):
            sl = pl.ds(n * TN, TN)
            part = _dot(ub[q, :, sl], w2[sl, :])
            tot = part if n == 0 else tot + part
        fo[r] = (acc + tot).astype(bf16)

        @pl.when(s < last)
        def _():
            sized(i, lambda: send_f(i, r, H).start(), lambda: send_f(i, r, C).start())

        @pl.when(s == last)
        def _():
            out_start(fo, r, i, fsem, s - 1)

        @pl.when(i > 0)
        def _():
            write_u(i).start()

        @pl.when(spill)
        def _():
            write_z(i).start()

            @pl.when(i == 4)
            def _():
                read_z(0).start()

    def backward(i, zw, dc):
        r = i % RING
        zs = jnp.where(spill, 2 + i % 2, i % 4)
        q = i % 2

        @pl.when(spill)
        def _():
            read_z(i).wait()
            ensure(write_z, zw, jnp.minimum(i + 2, n_ch))

            @pl.when(i + 1 < n_ch)
            def _():
                read_z(i + 1).start()

        ensure(write_d, dc, i - 1, 1)
        landed(gb, gsem, i)

        @pl.when(i >= RING)
        def _():
            @pl.when(s > 0)
            def _():
                sized(i - RING, lambda: send_b(i, r, H).wait_send(), lambda: send_b(i, r, C).wait_send())

            @pl.when(s == 0)
            def _():
                out_wait(bo, r, i - RING, bsem, s + 1)

        @pl.when(i == 0)
        def _():
            gb[end, low, :] = gb[0, top, :]

        gg = gb[i]
        for n in range(F // TN):
            sl = pl.ds(n * TN, TN)
            db[q, :, sl] = (zb[zs, :, sl] * _dot(gg, w2t[:, sl])).astype(bf16)
        for n in range(F // TN):
            sl = pl.ds(n * TN, TN)
            part = _dot(db[q, :, sl], w1t[sl, :])
            tot = part if n == 0 else tot + part
        bo[r] = (gg.astype(f32) + tot).astype(bf16)

        @pl.when(s > 0)
        def _():
            sized(i, lambda: send_b(i, r, H).start(), lambda: send_b(i, r, C).start())

        @pl.when(s == 0)
        def _():
            @pl.when(i == end)
            def _():
                for k in range(last, 2, -2):
                    direct(r, k).start()
            out_start(bo, r, i, bsem, s + 1)

        @pl.when(i > 0)
        def _():
            write_d(i).start()

    def prefetch(k, uc, dc):
        ensure(write_u, uc, 2 * k + 3, 1)
        ensure(write_d, dc, 2 * k + 3, 1)
        read_d(k).start()
        read_u(k).start()

    def weights(w):
        k = w // 2
        q = k % 2
        rows = pl.ds(2 * k + 1, 2)

        @pl.when(w % 2 == 0)
        def _():
            read_d(k).wait()
            h = hb[rows].reshape(2 * C, D)
            for n in range(F // TW):
                sl = pl.ds(n * TW, TW)
                a1[:, sl] += _dot_t(h, dw[q, :, sl])

        @pl.when(w % 2 == 1)
        def _():
            read_u(k).wait()
            gg = gb[rows].reshape(2 * C, D)
            for n in range(F // TW):
                sl = pl.ds(n * TW, TW)
                a2[sl, :] += _dot_t(uw[q, :, sl], gg)

    def relay_step(p):
        piece = rb.at[p]
        pltpu.make_async_copy(piece, piece, psem.at[p]).wait()

        @pl.when(even)
        def _():
            @pl.when(s >= 2)
            def _():
                onward(p, s - 2).start()

            @pl.when(s < n_st - 2)
            def _():
                across(p, s + 1).start()

        @pl.when(jnp.logical_not(even))
        def _():
            @pl.when((s < last) & (p < pieces - 1))
            def _():
                onward(p, s + 2).start()

            @pl.when(s > 1)
            def _():
                across(p, s - 1).start()

    def transposes():
        def f(n, _):
            sl = pl.ds(pl.multiple_of(n * 256, 256), 256)
            w1t[sl, :] = w1[:, sl].T
            w2t[:, sl] = w2[sl, :].T
            a1[:, sl] = jnp.zeros((D, 256), f32)
            a2[sl, :] = jnp.zeros((256, D), f32)
            return 0
        lax.fori_loop(0, F // 256, f, 0)

    def step(j, carry):
        word, nf, nb, nw, npf, nr, zw, uc, dc = carry
        op = word % 8
        is_f, is_b, is_p = op == 0, op == 1, op == 3

        @pl.when(is_f)
        def _():
            forward(nf, zw, uc)

        @pl.when(is_b)
        def _():
            backward(nb, zw, dc)

        @pl.when(op == 2)
        def _():
            weights(nw)

        @pl.when(is_p)
        def _():
            prefetch(npf, uc, dc)

        @pl.when(op == 4)
        def _():
            relay_step(nr)

        @pl.when(op == 5)
        def _():
            transposes()

        zw = jnp.where(is_f, jnp.maximum(zw, nf - 1), zw)
        zw = jnp.where(is_b, jnp.maximum(zw, jnp.minimum(nb + 2, n_ch)), zw)
        uc = jnp.where(is_f, jnp.maximum(uc, nf - 1), uc)
        uc = jnp.where(is_p, jnp.maximum(uc, 2 * npf + 3), uc)
        dc = jnp.where(is_b, jnp.maximum(dc, nb - 1), dc)
        dc = jnp.where(is_p, jnp.maximum(dc, 2 * npf + 3), dc)
        one = lambda k: jnp.where(op == k, 1, 0)
        return (word // 8, nf + one(0), nb + one(1), nw + one(2), npf + one(3), nr + one(4), zw, uc, dc)

    zero = s * 0
    words = []
    for k in range(len(WORDS[0])):
        word = zero
        for q in range(n_st):
            word = jnp.where(s == q, WORDS[q][k], word)
        words.append(word)

    def block(k, carry):
        word = words[0]
        for q in range(1, len(words)):
            word = jnp.where(k == q, words[q], word)
        out = lax.fori_loop(0, STEPS, step, (word, *carry))
        return out[1:]

    lax.fori_loop(0, len(words), block, (zero, zero, zero, zero, zero, zero, zero + 1, zero + 1))

    for j in range(RING):
        i = n_ch - RING + j
        r = i % RING
        rows = H if i == end else C

        @pl.when(s < last)
        def _(i=i, r=r, rows=rows):
            send_f(i, r, rows).wait_send()

        @pl.when(s == last)
        def _(i=i, r=r):
            out_wait(fo, r, i, fsem, s - 1)

        @pl.when(s > 0)
        def _(i=i, r=r, rows=rows):
            send_b(i, r, rows).wait_send()

        @pl.when(s == 0)
        def _(i=i, r=r):
            out_wait(bo, r, i, bsem, s + 1)

    @pl.when(s == 0)
    def _():
        for k in range(last, 2, -2):
            direct(end % RING, k).wait_send()

    def leaf(p):
        part = lf.at[p]
        pltpu.make_async_copy(part, part, lsem.at[1, p]).wait()

    def finish(p, _):
        @pl.when(even)
        def _():
            @pl.when(s >= 2)
            def _():
                onward(p, s - 2).wait_send()

            @pl.when(s < n_st - 2)
            def _():
                across(p, s + 1).wait_send()

            @pl.when(s > 0)
            def _():
                leaf(p)

        @pl.when(jnp.logical_not(even))
        def _():
            @pl.when((s < last) & (p < pieces - 1))
            def _():
                onward(p, s + 2).wait_send()

            @pl.when(s > 1)
            def _():
                across(p, s - 1).wait_send()

            @pl.when(s < last)
            def _():
                leaf(p)
        return 0
    lax.fori_loop(0, pieces, finish, 0)


def _write_out(lf, rb, a1, a2, y, dx, d1, d2, lb, sem_w, sem_r, sem_o):
    s = lax.axis_index("stage")
    parts = 4
    big = []
    for p in range(parts):
        r1 = pl.ds(p * (D // parts), D // parts)
        r2 = pl.ds(p * (F // parts), F // parts)
        big.append(pltpu.make_async_copy(a1.at[r1], d1.at[0, r1], sem_w.at[0, p]))
        big.append(pltpu.make_async_copy(a2.at[r2], d2.at[0, r2], sem_w.at[1, p]))
    back = pltpu.make_async_copy(lf, lb, sem_r)
    back.start()
    for c in big:
        c.start()

    def rest(mine, other):
        near = pltpu.make_async_copy(rb, mine, sem_o.at[0])
        near.start()
        back.wait()
        far = pltpu.make_async_copy(lb, other, sem_o.at[1])
        far.start()
        near.wait()
        far.wait()

    @pl.when(s % 2 == 0)
    def _():
        rest(y, dx)

    @pl.when(s % 2 == 1)
    def _():
        rest(dx, y)

    for c in big:
        c.wait()


def solution(mesh):
    n_st = mesh.shape["stage"]

    def body(x, g, w1, w2):
        tokens = x.shape[0] * x.shape[1]
        n_ch = tokens // C + 1
        hbm = pl.BlockSpec(memory_space=pltpu.HBM)
        vmem = pl.BlockSpec(memory_space=pltpu.VMEM)
        dma = pltpu.SemaphoreType.DMA
        pieces = (tokens // H, H, D)
        groups = (tokens // (2 * C), 2 * C, F)
        params = dict(has_side_effects=True)
        lf, rb, a1, a2, _, _, _ = pl.pallas_call(
            functools.partial(_pipeline, n_st, n_ch),
            out_shape=[pltpu.HBM(pieces, bf16), pltpu.VMEM(pieces, bf16), pltpu.VMEM((D, F), f32), pltpu.VMEM((F, D), f32),
                       pltpu.HBM((n_ch, C, F), f32), pltpu.HBM(groups, bf16), pltpu.HBM(groups, bf16)],
            in_specs=[hbm] * 4,
            out_specs=[hbm, vmem, vmem, vmem, hbm, hbm, hbm],
            scratch_shapes=[
                pltpu.VMEM((D, F), bf16), pltpu.VMEM((F, D), bf16), pltpu.VMEM((F, D), bf16), pltpu.VMEM((D, F), bf16),
                pltpu.VMEM((n_ch, C, D), bf16), pltpu.VMEM((n_ch, C, D), bf16), pltpu.VMEM((4, C, F), f32),
                pltpu.VMEM((2, C, F), bf16), pltpu.VMEM((2, C, F), bf16),
                pltpu.VMEM((2, 2 * C, F), bf16), pltpu.VMEM((2, 2 * C, F), bf16),
                pltpu.VMEM((RING, C, D), bf16), pltpu.VMEM((RING, C, D), bf16),
                dma((2,)), dma((n_ch,)), dma((n_ch,)), dma((pieces[0],)), dma((2, pieces[0])), dma((2, RING)), dma((2, RING)),
                dma((2, RING)), dma((2, pieces[0])), dma((2,)), dma((2,)), dma((2,)), dma((2,)), dma((2,)), dma((2,)),
            ],
            compiler_params=pltpu.CompilerParams(collective_id=0, vmem_limit_bytes=45_000_000, **params),
            name="pipeline",
        )(x.reshape(tokens, D), g.reshape(tokens, D), w1, w2)
        y, dx, d1, d2 = pl.pallas_call(
            _write_out,
            out_shape=[pltpu.HBM(pieces, bf16), pltpu.HBM(pieces, bf16), pltpu.HBM((1, D, F), f32), pltpu.HBM((1, F, D), f32)],
            in_specs=[hbm, vmem, vmem, vmem],
            out_specs=[hbm] * 4,
            scratch_shapes=[pltpu.VMEM(pieces, bf16), dma((2, 4)), dma, dma((2,))],
            compiler_params=pltpu.CompilerParams(vmem_limit_bytes=4_000_000, **params),
            name="write_out",
        )(pltpu.with_memory_space_constraint(lf, pltpu.HBM), rb, a1, a2)
        return y.reshape(x.shape), dx.reshape(x.shape), d1, d2

    return jax.shard_map(body, mesh=mesh,
                         in_specs=(P("data"), P("data"), P("stage"), P("stage")),
                         out_specs=(P("data"), P("data"), P(("data", "stage")), P(("data", "stage"))),
                         check_vma=False)
```

time: 163 us -> 151 us (0.926)
  Pallas kernels: 162 us -> 150 us
    pallas_call x1, Pallas kernels: 152 us -> 141 us  [body(): pl.pallas_call(functools.partial(_pipeline, n_st, n_ch), out_shape=[pltpu...]
where the time goes in v2:
time: 151 us
  Pallas kernels  150 us (99%)
    pallas_call x1, Pallas kernels, body(): pl.pallas_call(functools.partial(_pipeline, n_st, n_ch), out_shape=[pltpu...  141 us
    pallas_call x1, Pallas kernels, body(): pl.pallas_call(_write_out, out_shape=[pltpu.HBM(pieces, bf16), pltpu.HBM(...  8.98 us

profile of v2, /device:TPU:0, one launch (start us, length us, event | category | flops | bytes accessed | tf_op | source)
XLA Modules:
  0.0 150.7 jit_solution(14492392683859805420)
XLA Ops:
  0.6 141.1 %pipeline.1 = (bf16[32,64,768]{2,1,0:T(8,128)(2,1)}, bf16[32,64,768]{2,1,0:T(8,128)(2,1)S(1)}, f32[768,3072]{1,0:T(8,128)S(1)}, f32[3072,768]{1,0:T(8,128)S(1)},...) custom-call(bf16[2048,768]{1,0:T(8,128)(2,1)} %bitcast.4, ...), custom_call_target="tpu_custom_call" | custom-call | tf_op jit(solution)/shard_map/pipeline/pallas_call | solution.py:552
  141.7 9.0 %write_out.1 = (bf16[32,64,768]{2,1,0:T(8,128)(2,1)}, bf16[32,64,768]{2,1,0:T(8,128)(2,1)}, f32[1,768,3072]{2,1,0:T(8,128)}, f32[1,3072,768]{2,1,0:T(8,128)}) custom-call(bf16[32,64,768]{2,1,0:T(8,128)(2,1)} %get-tuple-element.12.lf, bf16[32,64,768]{2,1,0:T(8,128)(2,1)S(1)} %get-tuple-element.13.rb, f32[768,3072]{1,0:T(8,128)S(1)} %get-tuple-element.14.a1, ...), custom_call_target="tpu_custom_call" | custom-call | tf_op jit(solution)/shard_map/write_out/pallas_call | solution.py:570

commit v3 on v2

v3 whole, which is shorter than its diff:
```python
import functools

import jax
import jax.numpy as jnp
from jax import lax
from jax.experimental import pallas as pl
from jax.experimental.pallas import tpu as pltpu
from jax.sharding import PartitionSpec as P

MESH = pl.DeviceIdType.MESH
f32 = jnp.float32
bf16 = jnp.bfloat16
D = 768
F = 3072
C = 128
H = 64
RING = 4
K = 256
LAG = 6
TW = 512
NS = F // K
C0 = 0.7978845608028654
C1 = 0.044715

WORDS = (
    (0, 629145600, 606647049, 445683994, 579191882, 445686481, 292624673, 608807201, 580004132, 1073741820),
    (671088640, 150994944, 294754572, 575805217, 606749409, 613029986, 210126475, 608584482, 307050643, 1073741818),
    (5, 68159488, 158372612, 193282772, 189835348, 204576866, 575816290, 596265116, 608848026, 1073741818),
    (5, 151027712, 558211672, 191513249, 344267042, 611456268, 611358860, 340932770, 340867364, 1073741820),
    (8388613, 75515968, 142914081, 562315809, 292656394, 344245004, 592069916, 613497122, 307053850, 1073741818),
    (16777221, 19140672, 17045017, 591798945, 606411041, 579938532, 579942626, 478824604, 609364242, 1073741820),
    (545263877, 19927329, 201720577, 540020804, 193331969, 580008097, 579488028, 575482147, 308884690, 1073741818),
    (17043525, 17043521, 17043521, 612995137, 575743644, 328288036, 577390244, 610879780, 613566610, 1073741820),
)
STEPS = 10


def _dot(a, b):
    return jnp.dot(a, b, preferred_element_type=f32)


def _dot_t(a, b):
    return lax.dot_general(a, b, (((0,), (0,)), ((), ())), preferred_element_type=f32)


def _gelu(z):
    q = (C0 * C1) * (z * z)
    p = 0.5 * jnp.tanh(z * (C0 + q)) + 0.5
    u = z * p
    return u.astype(bf16), p + (u * (1.0 - p)) * (2.0 * C0 + 6.0 * q)


def _pipeline(n_st, n_ch, x, g, w1h, w2h, lf, rb, a1, a2, zh, uh, dh,
              w1, w2, w1t, w2t, hb, gb, zb, ub, db, uw, dw, fo, bo,
              wsem, hsem, gsem, psem, lsem, esem, fsem, bsem, osem, rsem, zwsem, zrsem, uwsem, dwsem, ursem, drsem):
    d = lax.axis_index("data")
    s = lax.axis_index("stage")
    last = n_st - 1
    end = n_ch - 1
    pieces = 2 * end
    spill = s < n_st - 2
    even = s % 2 == 0
    top, low = pl.ds(0, H), pl.ds(H, H)

    def peer(k):
        return (d, k)

    def sized(i, small, full):
        short = (i == 0) | (i == end)
        pl.when(short)(small)
        pl.when(jnp.logical_not(short))(full)

    def row(i):
        return jnp.maximum(i * C - H, 0)

    def cols(k):
        return pl.ds(k * K, K)

    def load(src, dst, sem, i):
        at = pl.ds(pl.multiple_of(row(i), H), C)
        return pltpu.make_async_copy(src.at[at], dst.at[i], sem.at[i])

    def load_end(src, dst, sem, i):
        at = pl.ds(0 if i == 0 else (2 * end - 1) * H, H)
        return pltpu.make_async_copy(src.at[at], dst.at[i, top], sem.at[i])

    def landed(buf, sem, i, rows):
        part = buf.at[i, pl.ds(0, rows)]
        pltpu.make_async_copy(part, part, sem.at[i]).wait()

    get_w1 = pltpu.make_async_copy(w1h.at[0], w1, wsem.at[0])
    get_w2 = pltpu.make_async_copy(w2h.at[0], w2, wsem.at[1])

    def load_all(src, dst, sem):
        load_end(src, dst, sem, end).start()

        def f(i, _):
            load(src, dst, sem, i).start()
            return 0
        lax.fori_loop(1, end, f, 0)

    @pl.when(s == 0)
    def _():
        load_end(x, hb, hsem, 0).start()

    get_w1.start()
    get_w2.start()

    @pl.when(s == 0)
    def _():
        load_all(x, hb, hsem)

    @pl.when(s == last)
    def _():
        load_end(g, gb, gsem, 0).start()
        load_all(g, gb, gsem)

    bar = pltpu.get_barrier_semaphore()
    near = (-2, -1, 1, 2)
    for off in near:
        @pl.when((s + off >= 0) & (s + off < n_st))
        def _(off=off):
            pl.semaphore_signal(bar, inc=1, device_id=peer(s + off), device_id_type=MESH)
    for k in range(3, n_st, 2):
        @pl.when(s == 0)
        def _(k=k):
            pl.semaphore_signal(bar, inc=1, device_id=peer(k), device_id_type=MESH)

        @pl.when(s == k)
        def _(k=k):
            pl.semaphore_signal(bar, inc=1, device_id=peer(0), device_id_type=MESH)
    far = jnp.where(s == 0, (n_st - 2) // 2, jnp.where((s % 2 == 1) & (s >= 3), 1, 0))
    peers = jnp.minimum(s, 2) + jnp.minimum(last - s, 2) + far

    def send(src, r, dst, i, ssem, to, dev, rows):
        part = pl.ds(0, rows)
        return pltpu.make_async_remote_copy(src_ref=src.at[r, part], dst_ref=dst.at[i, part], send_sem=ssem.at[0, r],
                                            recv_sem=to.at[i], device_id=peer(dev), device_id_type=MESH)

    def send_f(i, r, rows):
        return send(fo, r, hb, i, fsem, hsem, s + 1, rows)

    def send_b(i, r, rows):
        return send(bo, r, gb, i, bsem, gsem, s - 1, rows)

    def sent_f(i, r):
        sized(i, lambda: send_f(i, r, H).wait_send(), lambda: send_f(i, r, C).wait_send())

    def sent_b(i, r):
        sized(i, lambda: send_b(i, r, H).wait_send(), lambda: send_b(i, r, C).wait_send())

    def first_piece(i):
        return jnp.maximum(2 * i - 1, 0)

    def hand(src, r, k, p, ssem, dev):
        return pltpu.make_async_remote_copy(src_ref=src.at[r, pl.ds(k * H, H)], dst_ref=rb.at[p], send_sem=ssem.at[k, r],
                                            recv_sem=psem.at[p], device_id=peer(dev), device_id_type=MESH)

    def keep(src, r, k, p):
        return pltpu.make_async_copy(src.at[r, pl.ds(k * H, H)], lf.at[p], osem.at[k, r])

    def out_start(src, r, i, ssem, dev):
        p = first_piece(i)
        hand(src, r, 0, p, ssem, dev).start()
        keep(src, r, 0, p).start()

        def more():
            hand(src, r, 1, p + 1, ssem, dev).start()
            keep(src, r, 1, p + 1).start()
        sized(i, lambda: None, more)

    def out_wait(src, r, i, ssem, dev):
        p = first_piece(i)
        hand(src, r, 0, p, ssem, dev).wait_send()
        keep(src, r, 0, p).wait()

        def more():
            hand(src, r, 1, p + 1, ssem, dev).wait_send()
            keep(src, r, 1, p + 1).wait()
        sized(i, lambda: None, more)

    def direct(r, k):
        return pltpu.make_async_remote_copy(src_ref=bo.at[r, top], dst_ref=rb.at[pieces - 1], send_sem=esem.at[k // 2 - 1],
                                            recv_sem=psem.at[pieces - 1], device_id=peer(k), device_id_type=MESH)

    def onward(p, dev):
        return pltpu.make_async_remote_copy(src_ref=rb.at[p], dst_ref=rb.at[p], send_sem=rsem.at[0], recv_sem=psem.at[p],
                                            device_id=peer(dev), device_id_type=MESH)

    def across(p, dev):
        return pltpu.make_async_remote_copy(src_ref=rb.at[p], dst_ref=lf.at[p], send_sem=rsem.at[1], recv_sem=lsem,
                                            device_id=peer(dev), device_id_type=MESH)

    def write_z(i):
        q = lax.rem(i, 2)
        return pltpu.make_async_copy(zb.at[q], zh.at[i], zwsem.at[q])

    def read_z(i):
        q = lax.rem(i, 2)
        return pltpu.make_async_copy(zh.at[i], zb.at[2 + q], zrsem.at[q])

    def rows_of(i, rows):
        first = i == 0
        k = jnp.where(first, end // 2 - 1, lax.div(i - 1, 2))
        at = jnp.where(first, C + H, lax.rem(i - 1, 2) * C)
        return k, pl.ds(pl.multiple_of(at, H), rows)

    def write_ud(src, dst, sem, i, rows):
        k, at = rows_of(i, rows)
        q = lax.rem(i, 2)
        return pltpu.make_async_copy(src.at[q, pl.ds(0, rows)], dst.at[k, at], sem.at[q])

    def put_ud(src, dst, sem, i):
        sized(i, lambda: write_ud(src, dst, sem, i, H).start(), lambda: write_ud(src, dst, sem, i, C).start())

    def done_u(i):
        sized(i, lambda: write_ud(ub, uh, uwsem, i, H).wait(), lambda: write_ud(ub, uh, uwsem, i, C).wait())

    def done_d(i):
        sized(i, lambda: write_ud(db, dh, dwsem, i, H).wait(), lambda: write_ud(db, dh, dwsem, i, C).wait())

    def read_u(k):
        q = lax.rem(k, 2)
        return pltpu.make_async_copy(uh.at[k], uw.at[q], ursem.at[q])

    def read_d(k):
        q = lax.rem(k, 2)
        return pltpu.make_async_copy(dh.at[k], dw.at[q], drsem.at[q])

    def ensure(wait, done, want):
        for j in range(2):
            @pl.when(done + j < want)
            def _(j=j):
                wait(done + j)

    def forward_rows(i, r, zs, q, rows):
        landed(hb, hsem, i, rows)
        part = pl.ds(0, rows)
        h = hb[i, part, :]
        tot = None
        for n in range(NS + LAG):
            if n < NS:
                z = _dot(h, w1[:, cols(n)])
            if n >= LAG:
                m = n - LAG
                y = _dot(ub[q, part, cols(m)], w2[cols(m), :])
                tot = y if m == 0 else tot + y
            if n < NS:
                u, gp = _gelu(z)
                zb[zs, part, cols(n)] = gp
                ub[q, part, cols(n)] = u
        fo[r, part, :] = (h.astype(f32) + tot).astype(bf16)

        if rows == H:
            @pl.when(i == 0)
            def _():
                pl.semaphore_wait(bar, peers)

        @pl.when(s < last)
        def _():
            send_f(i, r, rows).start()

    def forward_end(i, r, zs, q, fresh):
        @pl.when(fresh)
        def _():
            get_w1.wait()
            get_w2.wait()

        forward_rows(i, r, zs, q, H)

        @pl.when(i == 0)
        def _():
            hb[end, low, :] = hb[0, top, :]

    def forward(i, zw, uc, fresh):
        r = lax.rem(i, RING)
        q = lax.rem(i, 2)
        zs = jnp.where(spill, q, lax.rem(i, 4))

        @pl.when(spill)
        def _():
            ensure(lambda j: write_z(j).wait(), zw, i - 1)

        ensure(done_u, uc, i - 1)

        @pl.when(i >= RING)
        def _():
            @pl.when(s < last)
            def _():
                sent_f(i - RING, r)

            @pl.when(s == last)
            def _():
                out_wait(fo, r, i - RING, fsem, s - 1)

        sized(i, lambda: forward_end(i, r, zs, q, fresh), lambda: forward_rows(i, r, zs, q, C))

        @pl.when(s == last)
        def _():
            out_start(fo, r, i, fsem, s - 1)

        put_ud(ub, uh, uwsem, i)

        @pl.when(spill)
        def _():
            write_z(i).start()

            @pl.when(i == 4)
            def _():
                read_z(0).start()

    def backward_rows(i, r, zs, q, rows):
        landed(gb, gsem, i, rows)
        part = pl.ds(0, rows)
        gg = gb[i, part, :]
        tot = None
        for n in range(NS + LAG):
            if n < NS:
                du = _dot(gg, w2t[:, cols(n)])
            if n >= LAG:
                m = n - LAG
                y = _dot(db[q, part, cols(m)], w1t[cols(m), :])
                tot = y if m == 0 else tot + y
            if n < NS:
                db[q, part, cols(n)] = (zb[zs, part, cols(n)] * du).astype(bf16)
        bo[r, part, :] = (gg.astype(f32) + tot).astype(bf16)

        @pl.when(s > 0)
        def _():
            send_b(i, r, rows).start()

    def backward_end(i, r, zs, q):
        backward_rows(i, r, zs, q, H)

        @pl.when(i == 0)
        def _():
            gb[end, low, :] = gb[0, top, :]

    def backward(i, zw, dc):
        r = lax.rem(i, RING)
        q = lax.rem(i, 2)
        zs = jnp.where(spill, 2 + q, lax.rem(i, 4))

        @pl.when(spill)
        def _():
            read_z(i).wait()
            ensure(lambda j: write_z(j).wait(), zw, jnp.minimum(i + 2, n_ch))

            @pl.when(i + 1 < n_ch)
            def _():
                read_z(i + 1).start()

        ensure(done_d, dc, i - 1)

        @pl.when(i >= RING)
        def _():
            @pl.when(s > 0)
            def _():
                sent_b(i - RING, r)

            @pl.when(s == 0)
            def _():
                out_wait(bo, r, i - RING, bsem, s + 1)

        sized(i, lambda: backward_end(i, r, zs, q), lambda: backward_rows(i, r, zs, q, C))

        @pl.when(s == 0)
        def _():
            @pl.when(i == end)
            def _():
                for k in range(last, 2, -2):
                    direct(r, k).start()
            out_start(bo, r, i, bsem, s + 1)

        put_ud(db, dh, dwsem, i)

    def prefetch(k, uc, dc):
        ensure(done_u, uc, 2 * k + 3)
        ensure(done_d, dc, 2 * k + 3)
        read_d(k).start()
        read_u(k).start()

    def weights(w):
        k = lax.div(w, 2)
        q = lax.rem(k, 2)
        rows = pl.ds(2 * k + 1, 2)
        odd = lax.rem(w, 2)

        @pl.when(odd == 0)
        def _():
            read_d(k).wait()
            h = hb[rows].reshape(2 * C, D)
            for n in range(F // TW):
                sl = pl.ds(n * TW, TW)
                a1[:, sl] += _dot_t(h, dw[q, :, sl])

        @pl.when(odd == 1)
        def _():
            read_u(k).wait()
            gg = gb[rows].reshape(2 * C, D)
            for n in range(F // TW):
                sl = pl.ds(n * TW, TW)
                a2[sl, :] += _dot_t(uw[q, :, sl], gg)

    def relay_step(p):
        piece = rb.at[p]
        pltpu.make_async_copy(piece, piece, psem.at[p]).wait()

        @pl.when(even)
        def _():
            @pl.when(s >= 2)
            def _():
                onward(p, s - 2).start()

            @pl.when(s < n_st - 2)
            def _():
                across(p, s + 1).start()

        @pl.when(jnp.logical_not(even))
        def _():
            @pl.when((s < last) & (p < pieces - 1))
            def _():
                onward(p, s + 2).start()

            @pl.when(s > 1)
            def _():
                across(p, s - 1).start()

    def transposes(fresh):
        @pl.when(fresh)
        def _():
            get_w1.wait()
            get_w2.wait()

        def f(n, _):
            sl = pl.ds(pl.multiple_of(n * 256, 256), 256)
            w1t[sl, :] = w1[:, sl].T
            w2t[:, sl] = w2[sl, :].T
            a1[:, sl] = jnp.zeros((D, 256), f32)
            a2[sl, :] = jnp.zeros((256, D), f32)
            return 0
        lax.fori_loop(0, F // 256, f, 0)

    def step(j, carry):
        word, nf, nb, nw, npf, nr, nt, zw, uc, dc = carry
        op = lax.rem(word, 8)
        is_f, is_b, is_p = op == 0, op == 1, op == 3

        @pl.when(op < 2)
        def _():
            @pl.when(is_f)
            def _():
                forward(nf, zw, uc, (nf == 0) & (nt == 0))

            @pl.when(is_b)
            def _():
                backward(nb, zw, dc)

        @pl.when(op >= 2)
        def _():
            @pl.when(op == 2)
            def _():
                weights(nw)

            @pl.when(op == 4)
            def _():
                relay_step(nr)

            @pl.when(is_p)
            def _():
                prefetch(npf, uc, dc)

            @pl.when(op == 5)
            def _():
                transposes(nf == 0)

        zw = jnp.where(is_f, jnp.maximum(zw, nf - 1), zw)
        zw = jnp.where(is_b, jnp.maximum(zw, jnp.minimum(nb + 2, n_ch)), zw)
        uc = jnp.where(is_f, jnp.maximum(uc, nf - 1), uc)
        uc = jnp.where(is_p, jnp.maximum(uc, 2 * npf + 3), uc)
        dc = jnp.where(is_b, jnp.maximum(dc, nb - 1), dc)
        dc = jnp.where(is_p, jnp.maximum(dc, 2 * npf + 3), dc)
        one = lambda k: jnp.where(op == k, 1, 0)
        return (lax.div(word, 8), nf + one(0), nb + one(1), nw + one(2), npf + one(3), nr + one(4), nt + one(5), zw, uc, dc)

    zero = s * 0
    words = []
    for k in range(len(WORDS[0])):
        word = zero
        for q in range(n_st):
            word = jnp.where(s == q, WORDS[q][k], word)
        words.append(word)

    def work(k, carry):
        word = words[0]
        for q in range(1, len(words)):
            word = jnp.where(k == q, words[q], word)
        out = lax.fori_loop(0, STEPS, step, (word, *carry))
        return out[1:]

    lax.fori_loop(0, len(words), work, (zero,) * 9)

    for j in range(RING):
        i = zero + (n_ch - RING + j)
        r = (n_ch - RING + j) % RING

        @pl.when(s < last)
        def _(i=i, r=r):
            sent_f(i, r)

        @pl.when(s == last)
        def _(i=i, r=r):
            out_wait(fo, r, i, fsem, s - 1)

        @pl.when(s > 0)
        def _(i=i, r=r):
            sent_b(i, r)

        @pl.when(s == 0)
        def _(i=i, r=r):
            out_wait(bo, r, i, bsem, s + 1)

    @pl.when(s == 0)
    def _():
        for k in range(last, 2, -2):
            direct(end % RING, k).wait_send()

    def all_of(ref, sem, count):
        part = ref.at[pl.ds(0, count)]
        pltpu.make_async_copy(part, part, sem).wait()

    @pl.when(even)
    def _():
        @pl.when(s >= 2)
        def _():
            all_of(rb, rsem.at[0], pieces)

        @pl.when(s < n_st - 2)
        def _():
            all_of(rb, rsem.at[1], pieces)

        @pl.when(s > 0)
        def _():
            all_of(lf, lsem, pieces)

    @pl.when(jnp.logical_not(even))
    def _():
        @pl.when(s < last)
        def _():
            all_of(rb, rsem.at[0], pieces - 1)
            all_of(lf, lsem, pieces)

        @pl.when(s > 1)
        def _():
            all_of(rb, rsem.at[1], pieces)


def _write_out(lf, rb, a1, a2, y, dx, d1, d2, lb, sem_w, sem_r, sem_o):
    s = lax.axis_index("stage")
    parts = 4
    big = []
    for p in range(parts):
        r1 = pl.ds(p * (D // parts), D // parts)
        r2 = pl.ds(p * (F // parts), F // parts)
        big.append(pltpu.make_async_copy(a1.at[r1], d1.at[0, r1], sem_w.at[0, p]))
        big.append(pltpu.make_async_copy(a2.at[r2], d2.at[0, r2], sem_w.at[1, p]))
    back = pltpu.make_async_copy(lf, lb, sem_r)
    back.start()
    for c in big:
        c.start()

    def rest(mine, other):
        near = pltpu.make_async_copy(rb, mine, sem_o.at[0])
        near.start()
        back.wait()
        far = pltpu.make_async_copy(lb, other, sem_o.at[1])
        far.start()
        near.wait()
        far.wait()

    @pl.when(s % 2 == 0)
    def _():
        rest(y, dx)

    @pl.when(s % 2 == 1)
    def _():
        rest(dx, y)

    for c in big:
        c.wait()


def solution(mesh):
    n_st = mesh.shape["stage"]

    def body(x, g, w1, w2):
        tokens = x.shape[0] * x.shape[1]
        n_ch = tokens // C + 1
        hbm = pl.BlockSpec(memory_space=pltpu.HBM)
        vmem = pl.BlockSpec(memory_space=pltpu.VMEM)
        dma = pltpu.SemaphoreType.DMA
        pieces = (tokens // H, H, D)
        groups = (tokens // (2 * C), 2 * C, F)
        params = dict(has_side_effects=True)
        lf, rb, a1, a2, _, _, _ = pl.pallas_call(
            functools.partial(_pipeline, n_st, n_ch),
            out_shape=[pltpu.HBM(pieces, bf16), pltpu.VMEM(pieces, bf16), pltpu.VMEM((D, F), f32), pltpu.VMEM((F, D), f32),
                       pltpu.HBM((n_ch, C, F), f32), pltpu.HBM(groups, bf16), pltpu.HBM(groups, bf16)],
            in_specs=[hbm] * 4,
            out_specs=[hbm, vmem, vmem, vmem, hbm, hbm, hbm],
            scratch_shapes=[
                pltpu.VMEM((D, F), bf16), pltpu.VMEM((F, D), bf16), pltpu.VMEM((F, D), bf16), pltpu.VMEM((D, F), bf16),
                pltpu.VMEM((n_ch, C, D), bf16), pltpu.VMEM((n_ch, C, D), bf16), pltpu.VMEM((4, C, F), f32),
                pltpu.VMEM((2, C, F), bf16), pltpu.VMEM((2, C, F), bf16),
                pltpu.VMEM((2, 2 * C, F), bf16), pltpu.VMEM((2, 2 * C, F), bf16),
                pltpu.VMEM((RING, C, D), bf16), pltpu.VMEM((RING, C, D), bf16),
                dma((2,)), dma((n_ch,)), dma((n_ch,)), dma((pieces[0],)), dma, dma((n_st // 2 - 1,)), dma((2, RING)), dma((2, RING)),
                dma((2, RING)), dma((2,)), dma((2,)), dma((2,)), dma((2,)), dma((2,)), dma((2,)), dma((2,)),
            ],
            compiler_params=pltpu.CompilerParams(collective_id=0, vmem_limit_bytes=45_000_000, **params),
            name="pipeline",
        )(x.reshape(tokens, D), g.reshape(tokens, D), w1, w2)
        y, dx, d1, d2 = pl.pallas_call(
            _write_out,
            out_shape=[pltpu.HBM(pieces, bf16), pltpu.HBM(pieces, bf16), pltpu.HBM((1, D, F), f32), pltpu.HBM((1, F, D), f32)],
            in_specs=[hbm, vmem, vmem, vmem],
            out_specs=[hbm] * 4,
            scratch_shapes=[pltpu.VMEM(pieces, bf16), dma((2, 4)), dma, dma((2,))],
            compiler_params=pltpu.CompilerParams(vmem_limit_bytes=4_000_000, **params),
            name="write_out",
        )(pltpu.with_memory_space_constraint(lf, pltpu.HBM), rb, a1, a2)
        return y.reshape(x.shape), dx.reshape(x.shape), d1, d2

    return jax.shard_map(body, mesh=mesh,
                         in_specs=(P("data"), P("data"), P("stage"), P("stage")),
                         out_specs=(P("data"), P("data"), P(("data", "stage")), P(("data", "stage"))),
                         check_vma=False)
```

time: 151 us -> 142 us (0.940)
  Pallas kernels: 150 us -> 141 us
    pallas_call x1, Pallas kernels: 141 us -> 132 us  [body(): pl.pallas_call(functools.partial(_pipeline, n_st, n_ch), out_shape=[pltpu...]
where the time goes in v3:
time: 142 us
  Pallas kernels  141 us (99%)
    pallas_call x1, Pallas kernels, body(): pl.pallas_call(functools.partial(_pipeline, n_st, n_ch), out_shape=[pltpu...  132 us
    pallas_call x1, Pallas kernels, body(): pl.pallas_call(_write_out, out_shape=[pltpu.HBM(pieces, bf16), pltpu.HBM(...  8.98 us

profile of v3, /device:TPU:0, one launch (start us, length us, event | category | flops | bytes accessed | tf_op | source)
XLA Modules:
  0.0 141.6 jit_solution(8555115660819920510)
XLA Ops:
  0.6 132.0 %pipeline.1 = (bf16[32,64,768]{2,1,0:T(8,128)(2,1)}, bf16[32,64,768]{2,1,0:T(8,128)(2,1)S(1)}, f32[768,3072]{1,0:T(8,128)S(1)}, f32[3072,768]{1,0:T(8,128)S(1)},...) custom-call(bf16[2048,768]{1,0:T(8,128)(2,1)} %bitcast.4, ...), custom_call_target="tpu_custom_call" | custom-call | tf_op jit(solution)/shard_map/pipeline/pallas_call | solution.py:605
  132.6 9.0 %write_out.1 = (bf16[32,64,768]{2,1,0:T(8,128)(2,1)}, bf16[32,64,768]{2,1,0:T(8,128)(2,1)}, f32[1,768,3072]{2,1,0:T(8,128)}, f32[1,3072,768]{2,1,0:T(8,128)}) custom-call(bf16[32,64,768]{2,1,0:T(8,128)(2,1)} %get-tuple-element.12.lf, bf16[32,64,768]{2,1,0:T(8,128)(2,1)S(1)} %get-tuple-element.13.rb, f32[768,3072]{1,0:T(8,128)S(1)} %get-tuple-element.14.a1, ...), custom_call_target="tpu_custom_call" | custom-call | tf_op jit(solution)/shard_map/write_out/pallas_call | solution.py:623

commit v4 on v3

--- a/solution.py
+++ b/solution.py
@@ -23,16 +23,16 @@
 C1 = 0.044715
 
 WORDS = (
-    (0, 629145600, 606647049, 445683994, 579191882, 445686481, 292624673, 608807201, 580004132, 1073741820),
-    (671088640, 150994944, 294754572, 575805217, 606749409, 613029986, 210126475, 608584482, 307050643, 1073741818),
-    (5, 68159488, 158372612, 193282772, 189835348, 204576866, 575816290, 596265116, 608848026, 1073741818),
-    (5, 151027712, 558211672, 191513249, 344267042, 611456268, 611358860, 340932770, 340867364, 1073741820),
-    (8388613, 75515968, 142914081, 562315809, 292656394, 344245004, 592069916, 613497122, 307053850, 1073741818),
-    (16777221, 19140672, 17045017, 591798945, 606411041, 579938532, 579942626, 478824604, 609364242, 1073741820),
-    (545263877, 19927329, 201720577, 540020804, 193331969, 580008097, 579488028, 575482147, 308884690, 1073741818),
-    (17043525, 17043521, 17043521, 612995137, 575743644, 328288036, 577390244, 610879780, 613566610, 1073741820),
+    (0, 0, 26230864, 20222273, 51647560, 37954580, 43192849, 36782609, 20070721, 159986706, 153633849, 268431945, 268435455),
+    (0, 0, 21038336, 69284929, 20517156, 54673988, 68293652, 51463234, 71450948, 71440660, 70337585, 54669956, 268435336),
+    (0, 67108864, 71319557, 68162628, 18953236, 26415426, 37831457, 21107473, 68232212, 71534915, 75711560, 142885955, 268435455),
+    (5, 0, 1118208, 21045523, 68424739, 26427793, 69282073, 68260417, 38020163, 70402617, 35865636, 260342596, 268435455),
+    (5, 67108928, 67387412, 26218516, 21106740, 34878465, 17908033, 36782402, 137662740, 69806403, 154289188, 35857027, 268435455),
+    (5, 1048592, 19927056, 1053458, 54599937, 43065665, 21074964, 69482563, 69419588, 52707908, 37962308, 71864900, 268435268),
+    (66640, 26251289, 73484550, 73687878, 1054278, 69407745, 38027585, 38028323, 37962308, 71508532, 58925602, 268435234, 268435455),
+    (100729093, 1054209, 16843009, 1052688, 70320385, 59909187, 76096553, 69481027, 70554162, 71443490, 153367620, 267993668, 268435455),
 )
-STEPS = 10
+STEPS = 7
 
 
 def _dot(a, b):
@@ -51,7 +51,7 @@
 
 
 def _pipeline(n_st, n_ch, x, g, w1h, w2h, lf, rb, a1, a2, zh, uh, dh,
-              w1, w2, w1t, w2t, hb, gb, zb, ub, db, uw, dw, fo, bo,
+              w1, w2, w1t, w2t, hb, gb, uw, dw, zb, ub, db, fo, bo,
               wsem, hsem, gsem, psem, lsem, esem, fsem, bsem, osem, rsem, zwsem, zrsem, uwsem, dwsem, ursem, drsem):
     d = lax.axis_index("data")
     s = lax.axis_index("stage")
@@ -210,9 +210,6 @@
         q = lax.rem(i, 2)
         return pltpu.make_async_copy(src.at[q, pl.ds(0, rows)], dst.at[k, at], sem.at[q])
 
-    def put_ud(src, dst, sem, i):
-        sized(i, lambda: write_ud(src, dst, sem, i, H).start(), lambda: write_ud(src, dst, sem, i, C).start())
-
     def done_u(i):
         sized(i, lambda: write_ud(ub, uh, uwsem, i, H).wait(), lambda: write_ud(ub, uh, uwsem, i, C).wait())
 
@@ -233,8 +230,35 @@
             def _(j=j):
                 wait(done + j)
 
-    def forward_rows(i, r, zs, q, rows):
-        landed(hb, hsem, i, rows)
+    def f_slots(i):
+        q = lax.rem(i, 2)
+        return lax.rem(i, RING), jnp.where(spill, q, lax.rem(i, 4)), q
+
+    def b_slots(i):
+        q = lax.rem(i, 2)
+        return lax.rem(i, RING), jnp.where(spill, 2 + q, lax.rem(i, 4)), q
+
+    def f_ready(i, zw, uc):
+        r, _, _ = f_slots(i)
+
+        @pl.when(spill)
+        def _():
+            ensure(lambda j: write_z(j).wait(), zw, i - 1)
+
+        ensure(done_u, uc, i - 1)
+
+        @pl.when(i >= RING)
+        def _():
+            @pl.when(s < last)
+            def _():
+                sent_f(i - RING, r)
+
+            @pl.when(s == last)
+            def _():
+                out_wait(fo, r, i - RING, fsem, s - 1)
+
+    def f_body(i, rows):
+        r, zs, q = f_slots(i)
         part = pl.ds(0, rows)
         h = hb[i, part, :]
         tot = None
@@ -251,128 +275,146 @@
                 ub[q, part, cols(n)] = u
         fo[r, part, :] = (h.astype(f32) + tot).astype(bf16)
 
-        if rows == H:
+    def f_first(i):
+        r, zs, q = f_slots(i)
+        get_w1.wait()
+        landed(hb, hsem, i, H)
+        h = hb[i, top, :]
+        for n in range(NS):
+            u, gp = _gelu(_dot(h, w1[:, cols(n)]))
+            zb[zs, top, cols(n)] = gp
+            ub[q, top, cols(n)] = u
+        get_w2.wait()
+        tot = None
+        for n in range(NS):
+            y = _dot(ub[q, top, cols(n)], w2[cols(n), :])
+            tot = y if n == 0 else tot + y
+        fo[r, top, :] = (h.astype(f32) + tot).astype(bf16)
+
+    def f_send(i, rows):
+        r, _, _ = f_slots(i)
+
+        @pl.when(s < last)
+        def _():
+            send_f(i, r, rows).start()
+
+        @pl.when(s == last)
+        def _():
+            out_start(fo, r, i, fsem, s - 1)
+
+        write_ud(ub, uh, uwsem, i, rows).start()
+
+        @pl.when(spill)
+        def _():
+            write_z(i).start()
+
+    def forward(i, zw, uc, fresh):
+        f_ready(i, zw, uc)
+
+        def small():
+            @pl.when(fresh)
+            def _():
+                f_first(i)
+
+            @pl.when(jnp.logical_not(fresh))
+            def _():
+                landed(hb, hsem, i, H)
+                f_body(i, H)
+
             @pl.when(i == 0)
             def _():
                 pl.semaphore_wait(bar, peers)
-
-        @pl.when(s < last)
-        def _():
-            send_f(i, r, rows).start()
-
-    def forward_end(i, r, zs, q, fresh):
-        @pl.when(fresh)
-        def _():
-            get_w1.wait()
-            get_w2.wait()
-
-        forward_rows(i, r, zs, q, H)
-
-        @pl.when(i == 0)
-        def _():
-            hb[end, low, :] = hb[0, top, :]
-
-    def forward(i, zw, uc, fresh):
-        r = lax.rem(i, RING)
-        q = lax.rem(i, 2)
-        zs = jnp.where(spill, q, lax.rem(i, 4))
+                hb[end, low, :] = hb[0, top, :]
+            f_send(i, H)
+
+        def full():
+            landed(hb, hsem, i, C)
+            f_body(i, C)
+            f_send(i, C)
+
+            @pl.when(spill & (i == 4))
+            def _():
+                read_z(0).start()
+        sized(i, small, full)
+
+    def b_ready(i, zw, dc):
+        r, _, _ = b_slots(i)
 
         @pl.when(spill)
         def _():
-            ensure(lambda j: write_z(j).wait(), zw, i - 1)
-
-        ensure(done_u, uc, i - 1)
+            read_z(i).wait()
+            ensure(lambda j: write_z(j).wait(), zw, jnp.minimum(i + 2, n_ch))
+
+            @pl.when(i + 1 < n_ch)
+            def _():
+                read_z(i + 1).start()
+
+        ensure(done_d, dc, i - 1)
 
         @pl.when(i >= RING)
         def _():
-            @pl.when(s < last)
-            def _():
-                sent_f(i - RING, r)
-
-            @pl.when(s == last)
-            def _():
-                out_wait(fo, r, i - RING, fsem, s - 1)
-
-        sized(i, lambda: forward_end(i, r, zs, q, fresh), lambda: forward_rows(i, r, zs, q, C))
-
-        @pl.when(s == last)
-        def _():
-            out_start(fo, r, i, fsem, s - 1)
-
-        put_ud(ub, uh, uwsem, i)
-
-        @pl.when(spill)
-        def _():
-            write_z(i).start()
-
-            @pl.when(i == 4)
-            def _():
-                read_z(0).start()
-
-    def backward_rows(i, r, zs, q, rows):
-        landed(gb, gsem, i, rows)
-        part = pl.ds(0, rows)
-        gg = gb[i, part, :]
+            @pl.when(s > 0)
+            def _():
+                sent_b(i - RING, r)
+
+            @pl.when(s == 0)
+            def _():
+                out_wait(bo, r, i - RING, bsem, s + 1)
+
+    def b_body(i):
+        r, zs, q = b_slots(i)
+        gg = gb[i]
         tot = None
         for n in range(NS + LAG):
             if n < NS:
                 du = _dot(gg, w2t[:, cols(n)])
             if n >= LAG:
                 m = n - LAG
-                y = _dot(db[q, part, cols(m)], w1t[cols(m), :])
+                y = _dot(db[q, :, cols(m)], w1t[cols(m), :])
                 tot = y if m == 0 else tot + y
             if n < NS:
-                db[q, part, cols(n)] = (zb[zs, part, cols(n)] * du).astype(bf16)
-        bo[r, part, :] = (gg.astype(f32) + tot).astype(bf16)
+                db[q, :, cols(n)] = (zb[zs, :, cols(n)] * du).astype(bf16)
+        bo[r] = (gg.astype(f32) + tot).astype(bf16)
+
+    def b_send(i, rows):
+        r, _, _ = b_slots(i)
 
         @pl.when(s > 0)
         def _():
             send_b(i, r, rows).start()
 
-    def backward_end(i, r, zs, q):
-        backward_rows(i, r, zs, q, H)
-
-        @pl.when(i == 0)
-        def _():
-            gb[end, low, :] = gb[0, top, :]
+        @pl.when(s == 0)
+        def _():
+            if rows == H:
+                @pl.when(i == end)
+                def _():
+                    for k in range(last, 2, -2):
+                        direct(r, k).start()
+            out_start(bo, r, i, bsem, s + 1)
+
+        write_ud(db, dh, dwsem, i, rows).start()
 
     def backward(i, zw, dc):
-        r = lax.rem(i, RING)
-        q = lax.rem(i, 2)
-        zs = jnp.where(spill, 2 + q, lax.rem(i, 4))
-
-        @pl.when(spill)
-        def _():
-            read_z(i).wait()
-            ensure(lambda j: write_z(j).wait(), zw, jnp.minimum(i + 2, n_ch))
-
-            @pl.when(i + 1 < n_ch)
-            def _():
-                read_z(i + 1).start()
-
-        ensure(done_d, dc, i - 1)
-
-        @pl.when(i >= RING)
-        def _():
-            @pl.when(s > 0)
-            def _():
-                sent_b(i - RING, r)
-
-            @pl.when(s == 0)
-            def _():
-                out_wait(bo, r, i - RING, bsem, s + 1)
-
-        sized(i, lambda: backward_end(i, r, zs, q), lambda: backward_rows(i, r, zs, q, C))
-
-        @pl.when(s == 0)
-        def _():
-            @pl.when(i == end)
-            def _():
-                for k in range(last, 2, -2):
-                    direct(r, k).start()
-            out_start(bo, r, i, bsem, s + 1)
-
-        put_ud(db, dh, dwsem, i)
+        b_ready(i, zw, dc)
+        sized(i, lambda: landed(gb, gsem, i, H), lambda: landed(gb, gsem, i, C))
+        b_body(i)
+
+        def small():
+            @pl.when(i == 0)
+            def _():
+                gb[end, low, :] = gb[0, top, :]
+            b_send(i, H)
+        sized(i, small, lambda: b_send(i, C))
+
+    def both(i, j, zw, uc, dc):
+        f_ready(i, zw, uc)
+        b_ready(j, jnp.maximum(zw, i - 1), dc)
+        landed(hb, hsem, i, C)
+        landed(gb, gsem, j, C)
+        f_body(i, C)
+        b_body(j)
+        b_send(j, C)
+        f_send(i, C)
 
     def prefetch(k, uc, dc):
         ensure(done_u, uc, 2 * k + 3)
@@ -380,27 +422,40 @@
         read_d(k).start()
         read_u(k).start()
 
+    def grad1(k):
+        q = lax.rem(k, 2)
+        h = hb[pl.ds(2 * k + 1, 2)].reshape(2 * C, D)
+        for n in range(F // TW):
+            sl = pl.ds(n * TW, TW)
+            a1[:, sl] += _dot_t(h, dw[q, :, sl])
+
+    def grad2(k):
+        q = lax.rem(k, 2)
+        gg = gb[pl.ds(2 * k + 1, 2)].reshape(2 * C, D)
+        for n in range(F // TW):
+            sl = pl.ds(n * TW, TW)
+            a2[sl, :] += _dot_t(uw[q, :, sl], gg)
+
     def weights(w):
         k = lax.div(w, 2)
-        q = lax.rem(k, 2)
-        rows = pl.ds(2 * k + 1, 2)
         odd = lax.rem(w, 2)
 
         @pl.when(odd == 0)
         def _():
             read_d(k).wait()
-            h = hb[rows].reshape(2 * C, D)
-            for n in range(F // TW):
-                sl = pl.ds(n * TW, TW)
-                a1[:, sl] += _dot_t(h, dw[q, :, sl])
+            grad1(k)
 
         @pl.when(odd == 1)
         def _():
             read_u(k).wait()
-            gg = gb[rows].reshape(2 * C, D)
-            for n in range(F // TW):
-                sl = pl.ds(n * TW, TW)
-                a2[sl, :] += _dot_t(uw[q, :, sl], gg)
+            grad2(k)
+
+    def weights_both(w):
+        k = lax.div(w, 2)
+        read_d(k).wait()
+        read_u(k).wait()
+        grad1(k)
+        grad2(k)
 
     def relay_step(p):
         piece = rb.at[p]
@@ -443,20 +498,21 @@
 
     def step(j, carry):
         word, nf, nb, nw, npf, nr, nt, zw, uc, dc = carry
-        op = lax.rem(word, 8)
-        is_f, is_b, is_p = op == 0, op == 1, op == 3
+        op = lax.rem(word, 16)
+        is_x = op == 6
+        is_f, is_b, is_p = (op == 0) | is_x, (op == 1) | is_x, op == 3
 
         @pl.when(op < 2)
         def _():
-            @pl.when(is_f)
+            @pl.when(op == 0)
             def _():
                 forward(nf, zw, uc, (nf == 0) & (nt == 0))
 
-            @pl.when(is_b)
+            @pl.when(op == 1)
             def _():
                 backward(nb, zw, dc)
 
-        @pl.when(op >= 2)
+        @pl.when((op >= 2) & (op < 6))
         def _():
             @pl.when(op == 2)
             def _():
@@ -473,6 +529,21 @@
             @pl.when(op == 5)
             def _():
                 transposes(nf == 0)
+
+        @pl.when(op >= 6)
+        def _():
+            @pl.when(is_x)
+            def _():
+                both(nf, nb, zw, uc, dc)
+
+            @pl.when(op == 8)
+            def _():
+                weights_both(nw)
+
+            @pl.when(op == 9)
+            def _():
+                relay_step(nr)
+                relay_step(nr + 1)
 
         zw = jnp.where(is_f, jnp.maximum(zw, nf - 1), zw)
         zw = jnp.where(is_b, jnp.maximum(zw, jnp.minimum(nb + 2, n_ch)), zw)
@@ -480,8 +551,10 @@
         uc = jnp.where(is_p, jnp.maximum(uc, 2 * npf + 3), uc)
         dc = jnp.where(is_b, jnp.maximum(dc, nb - 1), dc)
         dc = jnp.where(is_p, jnp.maximum(dc, 2 * npf + 3), dc)
-        one = lambda k: jnp.where(op == k, 1, 0)
-        return (lax.div(word, 8), nf + one(0), nb + one(1), nw + one(2), npf + one(3), nr + one(4), nt + one(5), zw, uc, dc)
+        one = lambda k: jnp.where(k, 1, 0)
+        two = lambda k, m: jnp.where(op == k, 1, jnp.where(op == m, 2, 0))
+        return (lax.div(word, 16), nf + one(is_f), nb + one(is_b), nw + two(2, 8), npf + one(is_p), nr + two(4, 9), nt + one(op == 5),
+                zw, uc, dc)
 
     zero = s * 0
     words = []
@@ -602,17 +675,18 @@
         pieces = (tokens // H, H, D)
         groups = (tokens // (2 * C), 2 * C, F)
         params = dict(has_side_effects=True)
+        rows = (n_ch, C, D)
+        slabs = (2, 2 * C, F)
         lf, rb, a1, a2, _, _, _ = pl.pallas_call(
             functools.partial(_pipeline, n_st, n_ch),
             out_shape=[pltpu.HBM(pieces, bf16), pltpu.VMEM(pieces, bf16), pltpu.VMEM((D, F), f32), pltpu.VMEM((F, D), f32),
                        pltpu.HBM((n_ch, C, F), f32), pltpu.HBM(groups, bf16), pltpu.HBM(groups, bf16)],
             in_specs=[hbm] * 4,
-            out_specs=[hbm, vmem, vmem, vmem, hbm, hbm, hbm],
+            out_specs=[hbm] + [vmem] * 3 + [hbm] * 3,
             scratch_shapes=[
                 pltpu.VMEM((D, F), bf16), pltpu.VMEM((F, D), bf16), pltpu.VMEM((F, D), bf16), pltpu.VMEM((D, F), bf16),
-                pltpu.VMEM((n_ch, C, D), bf16), pltpu.VMEM((n_ch, C, D), bf16), pltpu.VMEM((4, C, F), f32),
-                pltpu.VMEM((2, C, F), bf16), pltpu.VMEM((2, C, F), bf16),
-                pltpu.VMEM((2, 2 * C, F), bf16), pltpu.VMEM((2, 2 * C, F), bf16),
+                pltpu.VMEM(rows, bf16), pltpu.VMEM(rows, bf16), pltpu.VMEM(slabs, bf16), pltpu.VMEM(slabs, bf16),
+                pltpu.VMEM((4, C, F), f32), pltpu.VMEM((2, C, F), bf16), pltpu.VMEM((2, C, F), bf16),
                 pltpu.VMEM((RING, C, D), bf16), pltpu.VMEM((RING, C, D), bf16),
                 dma((2,)), dma((n_ch,)), dma((n_ch,)), dma((pieces[0],)), dma, dma((n_st // 2 - 1,)), dma((2, RING)), dma((2, RING)),
                 dma((2, RING)), dma((2,)), dma((2,)), dma((2,)), dma((2,)), dma((2,)), dma((2,)), dma((2,)),

time: 142 us -> 141 us (level)
  no operation moved by 1% of the time
where the time goes in v4:
time: 141 us
  Pallas kernels  141 us (100%)
    pallas_call x1, Pallas kernels, body(): pl.pallas_call(functools.partial(_pipeline, n_st, n_ch), out_shape=[pltpu...  132 us
    pallas_call x1, Pallas kernels, body(): pl.pallas_call(_write_out, out_shape=[pltpu.HBM(pieces, bf16), pltpu.HBM(...  8.98 us

profile of v4, /device:TPU:0, one launch (start us, length us, event | category | flops | bytes accessed | tf_op | source)
XLA Modules:
  0.0 141.2 jit_solution(1346717248794267617)
XLA Ops:
  0.6 131.6 %pipeline.1 = (bf16[32,64,768]{2,1,0:T(8,128)(2,1)}, bf16[32,64,768]{2,1,0:T(8,128)(2,1)S(1)}, f32[768,3072]{1,0:T(8,128)S(1)}, f32[3072,768]{1,0:T(8,128)S(1)},...) custom-call(bf16[2048,768]{1,0:T(8,128)(2,1)} %bitcast.4, ...), custom_call_target="tpu_custom_call" | custom-call | tf_op jit(solution)/shard_map/pipeline/pallas_call | solution.py:680
  132.2 9.0 %write_out.1 = (bf16[32,64,768]{2,1,0:T(8,128)(2,1)}, bf16[32,64,768]{2,1,0:T(8,128)(2,1)}, f32[1,768,3072]{2,1,0:T(8,128)}, f32[1,3072,768]{2,1,0:T(8,128)}) custom-call(bf16[32,64,768]{2,1,0:T(8,128)(2,1)} %get-tuple-element.12.lf, bf16[32,64,768]{2,1,0:T(8,128)(2,1)S(1)} %get-tuple-element.13.rb, f32[768,3072]{1,0:T(8,128)S(1)} %get-tuple-element.14.a1, ...), custom_call_target="tpu_custom_call" | custom-call | tf_op jit(solution)/shard_map/write_out/pallas_call | solution.py:697

commit v5 on v4

--- a/solution.py
+++ b/solution.py
@@ -18,19 +18,20 @@
 K = 256
 LAG = 6
 TW = 512
+SL = 3
 NS = F // K
 C0 = 0.7978845608028654
 C1 = 0.044715
 
 WORDS = (
-    (0, 0, 26230864, 20222273, 51647560, 37954580, 43192849, 36782609, 20070721, 159986706, 153633849, 268431945, 268435455),
-    (0, 0, 21038336, 69284929, 20517156, 54673988, 68293652, 51463234, 71450948, 71440660, 70337585, 54669956, 268435336),
-    (0, 67108864, 71319557, 68162628, 18953236, 26415426, 37831457, 21107473, 68232212, 71534915, 75711560, 142885955, 268435455),
-    (5, 0, 1118208, 21045523, 68424739, 26427793, 69282073, 68260417, 38020163, 70402617, 35865636, 260342596, 268435455),
-    (5, 67108928, 67387412, 26218516, 21106740, 34878465, 17908033, 36782402, 137662740, 69806403, 154289188, 35857027, 268435455),
-    (5, 1048592, 19927056, 1053458, 54599937, 43065665, 21074964, 69482563, 69419588, 52707908, 37962308, 71864900, 268435268),
-    (66640, 26251289, 73484550, 73687878, 1054278, 69407745, 38027585, 38028323, 37962308, 71508532, 58925602, 268435234, 268435455),
-    (100729093, 1054209, 16843009, 1052688, 70320385, 59909187, 76096553, 69481027, 70554162, 71443490, 153367620, 267993668, 268435455),
+    (0, 0, 17892608, 38016049, 18121010, 59905076, 17965348, 153171092, 19997076, 69481490, 75798915, 268387401, 268435455),
+    (0, 0, 21038336, 153172241, 71440675, 152322833, 37831730, 21053732, 34882116, 71383321, 70796337, 268404792, 268435455),
+    (5, 0, 71565316, 21038148, 71439121, 51462466, 54796865, 21107219, 70390337, 76820753, 155460132, 160662083, 268435234),
+    (0, 5242880, 16781328, 52502833, 69309457, 71385906, 68428098, 71573828, 26293281, 52707985, 71582276, 36254275, 268435332),
+    (5, 67108928, 21250068, 18092036, 17379728, 21039377, 54596424, 17908242, 70534212, 138691362, 54805033, 267944835, 268435455),
+    (5, 1048592, 50336016, 2167041, 51978257, 21107265, 71504708, 69485076, 35930948, 43136066, 71516745, 76096547, 268435268),
+    (66565, 151585092, 67702801, 1054992, 1052817, 20975641, 68423940, 71582532, 36848195, 153240626, 136520242, 253895219, 268435455),
+    (65797, 1052689, 16843009, 1052688, 16843009, 70395955, 43222073, 69411881, 160580754, 76751764, 76827010, 268435444, 268435455),
 )
 STEPS = 7
 
@@ -50,9 +51,15 @@
     return u.astype(bf16), p + (u * (1.0 - p)) * (2.0 * C0 + 6.0 * q)
 
 
-def _pipeline(n_st, n_ch, x, g, w1h, w2h, lf, rb, a1, a2, zh, uh, dh,
-              w1, w2, w1t, w2t, hb, gb, uw, dw, zb, ub, db, fo, bo,
-              wsem, hsem, gsem, psem, lsem, esem, fsem, bsem, osem, rsem, zwsem, zrsem, uwsem, dwsem, ursem, drsem):
+def _pipeline(n_st, n_ch, *refs):
+    dma = pltpu.SemaphoreType.DMA
+    pl.run_scoped(functools.partial(_work, n_st, n_ch, *refs), dma((2, SL)), dma((n_st // 2 - 1,)), dma((RING,)), dma((RING,)), dma((RING,)),
+                  dma((2,)), dma((2,)), dma((2,)), dma((2,)), dma((2,)), dma((2,)), dma((2,)))
+
+
+def _work(n_st, n_ch, x, g, w1h, w2h, lf, rb, a1, a2, zh, uh, dh,
+          w1, w2, w1t, w2t, hb, gb, uw, dw, zb, ub, db, fo, bo,
+          hsem, gsem, psem, lsem, wsem, esem, fsem, bsem, osem, rsem, zwsem, zrsem, uwsem, dwsem, ursem, drsem):
     d = lax.axis_index("data")
     s = lax.axis_index("stage")
     last = n_st - 1
@@ -88,8 +95,20 @@
         part = buf.at[i, pl.ds(0, rows)]
         pltpu.make_async_copy(part, part, sem.at[i]).wait()
 
-    get_w1 = pltpu.make_async_copy(w1h.at[0], w1, wsem.at[0])
-    get_w2 = pltpu.make_async_copy(w2h.at[0], w2, wsem.at[1])
+    def piece(n):
+        return pl.ds(n * (F // SL), F // SL)
+
+    def get_w1(n):
+        return pltpu.make_async_copy(w1h.at[0, :, piece(n)], w1.at[:, piece(n)], wsem.at[0, n])
+
+    def get_w2(n):
+        return pltpu.make_async_copy(w2h.at[0, piece(n)], w2.at[piece(n)], wsem.at[1, n])
+
+    def have_weights():
+        for n in range(SL):
+            get_w1(n).wait()
+        for n in range(SL):
+            get_w2(n).wait()
 
     def load_all(src, dst, sem):
         load_end(src, dst, sem, end).start()
@@ -103,8 +122,10 @@
     def _():
         load_end(x, hb, hsem, 0).start()
 
-    get_w1.start()
-    get_w2.start()
+    for n in range(SL):
+        get_w1(n).start()
+    for n in range(SL):
+        get_w2(n).start()
 
     @pl.when(s == 0)
     def _():
@@ -134,7 +155,7 @@
 
     def send(src, r, dst, i, ssem, to, dev, rows):
         part = pl.ds(0, rows)
-        return pltpu.make_async_remote_copy(src_ref=src.at[r, part], dst_ref=dst.at[i, part], send_sem=ssem.at[0, r],
+        return pltpu.make_async_remote_copy(src_ref=src.at[r, part], dst_ref=dst.at[i, part], send_sem=ssem.at[r],
                                             recv_sem=to.at[i], device_id=peer(dev), device_id_type=MESH)
 
     def send_f(i, r, rows):
@@ -153,11 +174,11 @@
         return jnp.maximum(2 * i - 1, 0)
 
     def hand(src, r, k, p, ssem, dev):
-        return pltpu.make_async_remote_copy(src_ref=src.at[r, pl.ds(k * H, H)], dst_ref=rb.at[p], send_sem=ssem.at[k, r],
+        return pltpu.make_async_remote_copy(src_ref=src.at[r, pl.ds(k * H, H)], dst_ref=rb.at[p], send_sem=ssem.at[r],
                                             recv_sem=psem.at[p], device_id=peer(dev), device_id_type=MESH)
 
     def keep(src, r, k, p):
-        return pltpu.make_async_copy(src.at[r, pl.ds(k * H, H)], lf.at[p], osem.at[k, r])
+        return pltpu.make_async_copy(src.at[r, pl.ds(k * H, H)], lf.at[p], osem.at[r])
 
     def out_start(src, r, i, ssem, dev):
         p = first_piece(i)
@@ -169,15 +190,12 @@
             keep(src, r, 1, p + 1).start()
         sized(i, lambda: None, more)
 
-    def out_wait(src, r, i, ssem, dev):
-        p = first_piece(i)
-        hand(src, r, 0, p, ssem, dev).wait_send()
-        keep(src, r, 0, p).wait()
-
-        def more():
-            hand(src, r, 1, p + 1, ssem, dev).wait_send()
-            keep(src, r, 1, p + 1).wait()
-        sized(i, lambda: None, more)
+    def out_wait(src, r, i, ssem):
+        def both(rows):
+            part = src.at[r, pl.ds(0, rows)]
+            pltpu.make_async_copy(part, part, ssem.at[r]).wait()
+            pltpu.make_async_copy(part, part, osem.at[r]).wait()
+        sized(i, lambda: both(H), lambda: both(C))
 
     def direct(r, k):
         return pltpu.make_async_remote_copy(src_ref=bo.at[r, top], dst_ref=rb.at[pieces - 1], send_sem=esem.at[k // 2 - 1],
@@ -238,9 +256,7 @@
         q = lax.rem(i, 2)
         return lax.rem(i, RING), jnp.where(spill, 2 + q, lax.rem(i, 4)), q
 
-    def f_ready(i, zw, uc):
-        r, _, _ = f_slots(i)
-
+    def f_ready(i, r, zw, uc):
         @pl.when(spill)
         def _():
             ensure(lambda j: write_z(j).wait(), zw, i - 1)
@@ -255,10 +271,10 @@
 
             @pl.when(s == last)
             def _():
-                out_wait(fo, r, i - RING, fsem, s - 1)
-
-    def f_body(i, rows):
-        r, zs, q = f_slots(i)
+                out_wait(fo, r, i - RING, fsem)
+
+    def f_body(i, rows, slots):
+        r, zs, q = slots
         part = pl.ds(0, rows)
         h = hb[i, part, :]
         tot = None
@@ -275,25 +291,25 @@
                 ub[q, part, cols(n)] = u
         fo[r, part, :] = (h.astype(f32) + tot).astype(bf16)
 
-    def f_first(i):
-        r, zs, q = f_slots(i)
-        get_w1.wait()
+    def f_first(i, slots):
+        r, zs, q = slots
         landed(hb, hsem, i, H)
         h = hb[i, top, :]
+        per = NS // SL
         for n in range(NS):
+            if n % per == 0:
+                get_w1(n // per).wait()
             u, gp = _gelu(_dot(h, w1[:, cols(n)]))
             zb[zs, top, cols(n)] = gp
             ub[q, top, cols(n)] = u
-        get_w2.wait()
         tot = None
-        for n in range(NS):
-            y = _dot(ub[q, top, cols(n)], w2[cols(n), :])
+        for n in range(SL):
+            get_w2(n).wait()
+            y = _dot(ub[q, top, piece(n)], w2[piece(n), :])
             tot = y if n == 0 else tot + y
         fo[r, top, :] = (h.astype(f32) + tot).astype(bf16)
 
-    def f_send(i, rows):
-        r, _, _ = f_slots(i)
-
+    def f_send(i, rows, r):
         @pl.when(s < last)
         def _():
             send_f(i, r, rows).start()
@@ -309,37 +325,37 @@
             write_z(i).start()
 
     def forward(i, zw, uc, fresh):
-        f_ready(i, zw, uc)
+        slots = f_slots(i)
+        r = slots[0]
+        f_ready(i, r, zw, uc)
 
         def small():
             @pl.when(fresh)
             def _():
-                f_first(i)
+                f_first(i, slots)
 
             @pl.when(jnp.logical_not(fresh))
             def _():
                 landed(hb, hsem, i, H)
-                f_body(i, H)
+                f_body(i, H, slots)
 
             @pl.when(i == 0)
             def _():
                 pl.semaphore_wait(bar, peers)
                 hb[end, low, :] = hb[0, top, :]
-            f_send(i, H)
+            f_send(i, H, r)
 
         def full():
             landed(hb, hsem, i, C)
-            f_body(i, C)
-            f_send(i, C)
+            f_body(i, C, slots)
+            f_send(i, C, r)
 
             @pl.when(spill & (i == 4))
             def _():
                 read_z(0).start()
         sized(i, small, full)
 
-    def b_ready(i, zw, dc):
-        r, _, _ = b_slots(i)
-
+    def b_ready(i, r, zw, dc):
         @pl.when(spill)
         def _():
             read_z(i).wait()
@@ -359,10 +375,10 @@
 
             @pl.when(s == 0)
             def _():
-                out_wait(bo, r, i - RING, bsem, s + 1)
-
-    def b_body(i):
-        r, zs, q = b_slots(i)
+                out_wait(bo, r, i - RING, bsem)
+
+    def b_body(i, slots):
+        r, zs, q = slots
         gg = gb[i]
         tot = None
         for n in range(NS + LAG):
@@ -376,9 +392,7 @@
                 db[q, :, cols(n)] = (zb[zs, :, cols(n)] * du).astype(bf16)
         bo[r] = (gg.astype(f32) + tot).astype(bf16)
 
-    def b_send(i, rows):
-        r, _, _ = b_slots(i)
-
+    def b_send(i, rows, r):
         @pl.when(s > 0)
         def _():
             send_b(i, r, rows).start()
@@ -395,26 +409,24 @@
         write_ud(db, dh, dwsem, i, rows).start()
 
     def backward(i, zw, dc):
-        b_ready(i, zw, dc)
-        sized(i, lambda: landed(gb, gsem, i, H), lambda: landed(gb, gsem, i, C))
-        b_body(i)
+        slots = b_slots(i)
+        r = slots[0]
+        b_ready(i, r, zw, dc)
 
         def small():
+            landed(gb, gsem, i, H)
+            b_body(i, slots)
+
             @pl.when(i == 0)
             def _():
                 gb[end, low, :] = gb[0, top, :]
-            b_send(i, H)
-        sized(i, small, lambda: b_send(i, C))
-
-    def both(i, j, zw, uc, dc):
-        f_ready(i, zw, uc)
-        b_ready(j, jnp.maximum(zw, i - 1), dc)
-        landed(hb, hsem, i, C)
-        landed(gb, gsem, j, C)
-        f_body(i, C)
-        b_body(j)
-        b_send(j, C)
-        f_send(i, C)
+            b_send(i, H, r)
+
+        def full():
+            landed(gb, gsem, i, C)
+            b_body(i, slots)
+            b_send(i, C, r)
+        sized(i, small, full)
 
     def prefetch(k, uc, dc):
         ensure(done_u, uc, 2 * k + 3)
@@ -482,10 +494,7 @@
                 across(p, s - 1).start()
 
     def transposes(fresh):
-        @pl.when(fresh)
-        def _():
-            get_w1.wait()
-            get_w2.wait()
+        pl.when(fresh)(have_weights)
 
         def f(n, _):
             sl = pl.ds(pl.multiple_of(n * 256, 256), 256)
@@ -499,16 +508,15 @@
     def step(j, carry):
         word, nf, nb, nw, npf, nr, nt, zw, uc, dc = carry
         op = lax.rem(word, 16)
-        is_x = op == 6
-        is_f, is_b, is_p = (op == 0) | is_x, (op == 1) | is_x, op == 3
+        is_f, is_b, is_p = op == 0, op == 1, op == 3
 
         @pl.when(op < 2)
         def _():
-            @pl.when(op == 0)
+            @pl.when(is_f)
             def _():
                 forward(nf, zw, uc, (nf == 0) & (nt == 0))
 
-            @pl.when(op == 1)
+            @pl.when(is_b)
             def _():
                 backward(nb, zw, dc)
 
@@ -532,10 +540,6 @@
 
         @pl.when(op >= 6)
         def _():
-            @pl.when(is_x)
-            def _():
-                both(nf, nb, zw, uc, dc)
-
             @pl.when(op == 8)
             def _():
                 weights_both(nw)
@@ -583,7 +587,7 @@
 
         @pl.when(s == last)
         def _(i=i, r=r):
-            out_wait(fo, r, i, fsem, s - 1)
+            out_wait(fo, r, i, fsem)
 
         @pl.when(s > 0)
         def _(i=i, r=r):
@@ -591,7 +595,7 @@
 
         @pl.when(s == 0)
         def _(i=i, r=r):
-            out_wait(bo, r, i, bsem, s + 1)
+            out_wait(bo, r, i, bsem)
 
     @pl.when(s == 0)
     def _():
@@ -688,8 +692,7 @@
                 pltpu.VMEM(rows, bf16), pltpu.VMEM(rows, bf16), pltpu.VMEM(slabs, bf16), pltpu.VMEM(slabs, bf16),
                 pltpu.VMEM((4, C, F), f32), pltpu.VMEM((2, C, F), bf16), pltpu.VMEM((2, C, F), bf16),
                 pltpu.VMEM((RING, C, D), bf16), pltpu.VMEM((RING, C, D), bf16),
-                dma((2,)), dma((n_ch,)), dma((n_ch,)), dma((pieces[0],)), dma, dma((n_st // 2 - 1,)), dma((2, RING)), dma((2, RING)),
-                dma((2, RING)), dma((2,)), dma((2,)), dma((2,)), dma((2,)), dma((2,)), dma((2,)), dma((2,)),
+                dma((n_ch,)), dma((n_ch,)), dma((pieces[0],)), dma,
             ],
             compiler_params=pltpu.CompilerParams(collective_id=0, vmem_limit_bytes=45_000_000, **params),
             name="pipeline",

time: 141 us -> 141 us (level)
  Pallas kernels: 141 us -> 139 us
where the time goes in v5:
time: 141 us; the launch traced here: 140 us
  Pallas kernels  139 us (99%)
    pallas_call x1, Pallas kernels, body(): pl.pallas_call(functools.partial(_pipeline, n_st, n_ch), out_shape=[pltpu...  130 us
    pallas_call x1, Pallas kernels, body(): pl.pallas_call(_write_out, out_shape=[pltpu.HBM(pieces, bf16), pltpu.HBM(...  8.98 us

profile of v5, /device:TPU:0, one launch (start us, length us, event | category | flops | bytes accessed | tf_op | source)
XLA Modules:
  0.0 140.1 jit_solution(4241656703486293985)
XLA Ops:
  0.6 130.4 %pipeline.1 = (bf16[32,64,768]{2,1,0:T(8,128)(2,1)}, bf16[32,64,768]{2,1,0:T(8,128)(2,1)S(1)}, f32[768,3072]{1,0:T(8,128)S(1)}, f32[3072,768]{1,0:T(8,128)S(1)},...) custom-call(bf16[2048,768]{1,0:T(8,128)(2,1)} %bitcast.4, ...), custom_call_target="tpu_custom_call" | custom-call | tf_op jit(solution)/shard_map/pipeline/pallas_call | solution.py:684
  131.1 9.0 %write_out.1 = (bf16[32,64,768]{2,1,0:T(8,128)(2,1)}, bf16[32,64,768]{2,1,0:T(8,128)(2,1)}, f32[1,768,3072]{2,1,0:T(8,128)}, f32[1,3072,768]{2,1,0:T(8,128)}) custom-call(bf16[32,64,768]{2,1,0:T(8,128)(2,1)} %get-tuple-element.12.lf, bf16[32,64,768]{2,1,0:T(8,128)(2,1)S(1)} %get-tuple-element.13.rb, f32[768,3072]{1,0:T(8,128)S(1)} %get-tuple-element.14.a1, ...), custom_call_target="tpu_custom_call" | custom-call | tf_op jit(solution)/shard_map/write_out/pallas_call | solution.py:700
